TPU v7x, 128 devices: a whole 4x4x4 slice. The times are simulated.
128 devices in a mesh: blk: 64 (over x, y, z_lo, core), grp: 2 (over z_hi).
Axes of the slice: x: 4, y: 4, z: 4 (z_hi: 2, z_lo: 2; z = z_hi * 2 + z_lo), core: 2. Of those that a mesh axis runs over, the one named last changes fastest.
Arguments:
- sky_maps: float32 [4, 512, 4096], P(None, ('blk', 'grp')), may hold values from -6 to 6
- legendre: bfloat16 [512, 512, 2048], P(('blk', 'grp')), may hold values from -0.25 to 0.25
- owner_table: int32 [512], replicated, may hold values from 0 to 511, each once
Outputs:
- harmonics: float32 [512, 4, 2, 2048], P(('blk', 'grp'))
- spectra: float32 [10, 2048], P(None, ('blk', 'grp'))
Inputs may be any that keep to these rules, and one draw needn't show every extreme that they name: `owner_table`: a permutation of the orders 0 to 511.
All inputs are finite; a program needn't handle non-finite values.
Results may differ from a plain program's by a relative error of at most 0.0034.
Values may be sent and summed in bfloat16 or wider, within the bound.
A program may use at most 128 MiB of HBM per device.

v0:
```python
import functools
import math

import jax
import jax.numpy as jnp
import numpy as np
from jax import lax
from jax.experimental import pallas as pl
from jax.experimental.pallas import tpu as pltpu
from jax.sharding import PartitionSpec as P

MESH = pl.DeviceIdType.MESH
F32 = jnp.float32
BF16 = jnp.bfloat16
UNITS = 16
PARTS = 6
LANES = 128


def iota(shape, dim):
    return lax.broadcasted_iota(jnp.int32, shape, dim)


def dft_tables():
    k2 = np.arange(128)[:, None]
    m = np.arange(512)[None, :]
    angle = 2.0 * math.pi * ((k2 * m) % 4096) / 4096.0
    table = np.concatenate([np.cos(angle), -np.sin(angle)], axis=1) / 64.0
    k1 = np.arange(32)[:, None]
    turn = 2.0 * math.pi * ((k1 * m) % 32) / 32.0
    twiddle = np.stack([np.cos(turn), np.sin(turn)], axis=1)
    return table.astype(np.float32), twiddle.astype(np.float32)


def kernel(
    sky_ref, leg_ref, own_ref, table_ref, twid_ref, harm_ref, spec_ref,
    legv, sendb, recvb, perm, hot, amat, fx, fz, fre, fown, frecv,
    acc, passb, passr, acc2, s2, r2, acc3, s3, r3, sp1, r1s, sp2, r2s, morder, mweight,
    leg_sem, a_send, a_recv, f_send, f_recv, b_send, b_recv, c_send, c_recv,
    d_send, d_recv, e_send, e_recv, g_send, g_recv,
):
    blk = lax.axis_index("blk")
    grp = lax.axis_index("grp")
    x = blk // 16
    y = (blk // 4) % 4
    z = grp * 2 + (blk // 2) % 2
    core = blk % 2

    def pick(axis, v0, v1, v2):
        return jnp.where(axis == 0, v0, jnp.where(axis == 1, v1, v2))

    def coords(axis):
        return pick(axis, x, y, z), pick(axis, y, z, x), pick(axis, z, x, y)

    def device(xx, yy, zz, cc):
        return (xx * 16 + yy * 4 + (zz % 2) * 2 + cc, zz // 2)

    def at(axis, v1, v2, v3, cc):
        return device(pick(axis, v1, v3, v2), pick(axis, v2, v1, v3), pick(axis, v3, v2, v1), cc)

    def part_of(u):
        part = u % PARTS
        return part, part // 2, part % 2

    def pairs(axis, par):
        a1, a2, a3 = coords(axis)
        step = (1 - 2 * (a1 % 2)) * (1 - 2 * par)
        first = (a1 + step + 4) % 4
        second = (a1 - step + 4) % 4
        return a1, a2, a3, first, second

    def remote(src, dst, ss, rs, dev):
        return pltpu.make_async_remote_copy(
            src_ref=src, dst_ref=dst, send_sem=ss, recv_sem=rs, device_id=dev, device_id_type=MESH
        )

    def loop(lo, hi, f):
        def body(i, c):
            f(i)
            return c

        lax.fori_loop(lo, hi, body, 0)

    def leg_copy(u):
        lanes = pl.ds(pl.multiple_of(u * LANES, LANES), LANES)
        return pltpu.make_async_copy(leg_ref.at[:, :, lanes], legv.at[u], leg_sem.at[u])

    loop(0, UNITS, lambda u: leg_copy(u).start())

    def hot_rows(i):
        rows = pl.ds(pl.multiple_of(i * 128, 128), 128)
        same = iota((128, 512), 0) + i * 128 == own_ref[...]
        hot[rows, :] = jnp.where(same, 1.0, 0.0).astype(BF16)

    loop(0, 4, hot_rows)

    def perm_rows(axis):
        a1, a2, a3 = coords(axis)
        step = 1 - 2 * (a1 % 2)
        i = iota((512, 512), 0)
        j = i & 3
        v3 = (a3 + (i >> 2)) & 3
        v2 = (a2 + (i >> 4)) & 3
        cc = core ^ ((i >> 6) & 1)
        v1 = (a1 + ((i >> 7) + 1) * step + 16) & 3
        xx = pick(axis, v1, v3, v2)
        yy = pick(axis, v2, v1, v3)
        zz = pick(axis, v3, v2, v1)
        slot = ((((xx * 4 + yy) * 2 + (zz & 1)) * 2 + cc) * 2 + (zz >> 1)) * 4 + j
        chosen = jnp.where(slot == iota((512, 512), 1), 1.0, 0.0).astype(BF16)
        rows = lax.dot_general(
            chosen, hot[...], (((1,), (1,)), ((), ())), preferred_element_type=F32
        )
        perm[axis] = rows.astype(BF16)

    loop(0, 3, perm_rows)

    def a_copies(u):
        part, axis, par = part_of(u)
        a1, a2, a3, first, _ = pairs(axis, par)
        return (
            remote(sendb.at[u, 1, pl.ds(2, 2)], recvb.at[u, 0], a_send.at[u, 0], a_recv.at[u, 0],
                   at(axis, a1, a2, a3, 1 - core)),
            remote(sendb.at[u, 0, pl.ds(0, 2)], recvb.at[u, 1], a_send.at[u, 1], a_recv.at[u, 1],
                   at(axis, first, a2, a3, core)),
            remote(sendb.at[u, 1, pl.ds(0, 2)], recvb.at[u, 2], a_send.at[u, 2], a_recv.at[u, 2],
                   at(axis, first, a2, a3, 1 - core)),
        )

    def phase_a(u):
        part, axis, par = part_of(u)
        leg_copy(u).wait()
        roles = (3 * par, 1, 3 - 3 * par, 2)
        for pair in range(2):
            wide = jnp.concatenate([legv[u, 2 * pair], legv[u, 2 * pair + 1]], axis=1)
            rows = jnp.dot(perm[axis], wide, preferred_element_type=F32).astype(BF16)
            for rel in range(4):
                for rc in range(2):
                    piece = rows[rel * 128 + rc * 64 : rel * 128 + rc * 64 + 64]
                    sendb[u, rc, roles[rel], 2 * pair] = piece[:, :128]
                    sendb[u, rc, roles[rel], 2 * pair + 1] = piece[:, 128:]
        for copy in a_copies(u):
            copy.start()

    def fourier():
        for a in range(4):
            for k1 in range(32):
                fx[k1 * 16 + a * 4 : k1 * 16 + a * 4 + 4, :] = sky_ref[
                    a, :, k1 * 128 : (k1 + 1) * 128
                ]

        def rows_of(i):
            rows = pl.ds(pl.multiple_of(i * 128, 128), 128)
            fz[rows, :] = jnp.dot(
                fx[rows, :], table_ref[...], precision=lax.Precision.HIGHEST,
                preferred_element_type=F32,
            )

        loop(0, 4, rows_of)

        def add(k1, sums):
            re, im = sums
            rows = pl.ds(pl.multiple_of(k1 * 16, 16), 16)
            zr = fz[rows, 0:512]
            zi = fz[rows, 512:1024]
            c = twid_ref[k1, 0:1, :]
            s = twid_ref[k1, 1:2, :]
            return re + (zr * c + zi * s), im + (zi * c - zr * s)

        zero = jnp.zeros((16, 512), F32)
        re, im = lax.fori_loop(0, 32, add, (zero, zero))
        fre[0] = re
        fre[1] = im
        for r in range(4):
            rows = [fre[q, a * 4 + r : a * 4 + r + 1, :] for a in range(4) for q in range(2)]
            fown[r * 8 : r * 8 + 8, :] = jnp.concatenate(rows, axis=0).astype(BF16)

    def f_first():
        return remote(fown, frecv.at[0], f_send.at[0], f_recv.at[0], device(x, y, z, 1 - core))

    def f_copies(part):
        a1, a2, a3, first, _ = pairs(part // 2, part % 2)
        return [
            remote(fown, frecv.at[1 + 2 * part + k], f_send.at[1 + 2 * part + k],
                   f_recv.at[1 + 2 * part + k], at(part // 2, first, a2, a3, core ^ k))
            for k in range(2)
        ]

    def f_start(part):
        for copy in f_copies(part):
            copy.start()

    def build(part):
        axis, par = part // 2, part % 2
        for copy in f_copies(part):
            copy.wait_recv()
        four = jnp.concatenate(
            [fown[...], frecv[0], frecv[1 + 2 * part], frecv[2 + 2 * part]], axis=0
        )
        passed = pl.multiple_of((2 - 2 * par) * 128, 128)
        mine = jnp.concatenate([perm[axis, 384:448, :], perm[axis, pl.ds(passed, 64), :]], axis=0)
        picked = lax.dot_general(
            four, mine, (((1,), (1,)), ((), ())), preferred_element_type=F32
        ).astype(BF16)
        lane = iota((128, 1024), 1)
        spread = (lane >> 7) * 16 + (lane & 15) == iota((128, 1024), 0)
        tiled = jnp.dot(
            picked, jnp.where(spread, 1.0, 0.0).astype(BF16), preferred_element_type=F32
        )
        group = iota((8, 128), 1) >> 4
        diagonal = (iota((128, 128), 0) >> 3) == (iota((128, 128), 1) & 15)
        for g in range(8):
            for h in range(2):
                base = jnp.zeros((8, 128), F32)
                for i in range(8):
                    row = (8 * h + i) * 8
                    base = jnp.where(
                        group == i, tiled[row : row + 8, g * 128 : g * 128 + 128], base
                    )
                full = jnp.concatenate([base] * 16, axis=0)
                amat[part, g, :, h * 128 : h * 128 + 128] = jnp.where(diagonal, full, 0.0).astype(
                    BF16
                )

    def b_copy(u):
        part, axis, par = part_of(u)
        _, a2, a3, _, second = pairs(axis, par)
        return remote(passb.at[u], passr.at[u], b_send.at[u], b_recv.at[u],
                      at(axis, second, a2, a3, core))

    def phase_b(u):
        part, axis, par = part_of(u)
        for copy in a_copies(u):
            copy.wait_recv()
        for g in range(8):
            sub, low = g // 4, 16 * (g % 4)
            slabs = [sendb[u, 0, 2 + sub, r, low : low + 16, :] for r in range(4)]
            for src in range(3):
                slabs += [recvb[u, src, sub, r, low : low + 16, :] for r in range(4)]
            out = jnp.dot(
                amat[part, g], jnp.concatenate(slabs, axis=0), preferred_element_type=F32
            )
            rows = slice((g % 4) * 128, (g % 4) * 128 + 128)
            if sub == 0:
                acc[u, rows, :] = out
            else:
                passb[u, rows, :] = out.astype(BF16)
        b_copy(u).start()

    def c_copies(u):
        part, axis, par = part_of(u)
        a1, a2, a3 = coords(axis)
        return [
            remote(s2.at[u, d], r2.at[u, d], c_send.at[u, d], c_recv.at[u, d],
                   at(axis, a1, (a2 + d + 1) % 4, a3, core))
            for d in range(3)
        ]

    def phase_c(u):
        b_copy(u).wait_recv()
        for d in range(4):
            rows = slice(d * 128, d * 128 + 128)
            total = acc[u, rows, :] + passr[u, rows, :].astype(F32)
            if d == 0:
                acc2[u] = total
            else:
                s2[u, d - 1] = total.astype(BF16)
        for copy in c_copies(u):
            copy.start()

    def d_copies(u):
        part, axis, par = part_of(u)
        a1, a2, a3 = coords(axis)
        return [
            remote(s3.at[u, d], r3.at[u, d], d_send.at[u, d], d_recv.at[u, d],
                   at(axis, a1, a2, (a3 + d + 1) % 4, core))
            for d in range(3)
        ]

    def phase_d(u):
        for copy in c_copies(u):
            copy.wait_recv()
        total = acc2[u]
        for d in range(3):
            total = total + r2[u, d].astype(F32)
        acc3[u] = total[0:32]
        for d in range(3):
            s3[u, d] = total[32 * d + 32 : 32 * d + 64]
        for copy in d_copies(u):
            copy.start()

    column = x * 4 + y
    place = z * 2 + core

    def e_copy(u):
        target = u // 2
        return remote(sp1.at[u], r1s.at[u % 2, place], e_send.at[u], e_recv.at[u % 2, place],
                      device(x, y, target // 2, target % 2))

    def phase_e(u):
        for copy in d_copies(u):
            copy.wait_recv()
        total = acc3[u]
        for d in range(3):
            total = total + r3[u, d]
        ell = (u * LANES + iota((32, 128), 1)).astype(F32)
        total = jnp.where(ell >= morder[...], total, 0.0)
        harm_ref[:, pl.ds(pl.multiple_of(u * LANES, LANES), LANES)] = total
        heavy = total * mweight[...]
        near = [jnp.zeros((8, 128), F32) for _ in range(3)]
        for j in range(4):
            one = total[8 * j : 8 * j + 8]
            weighted = heavy[8 * j : 8 * j + 8]
            for k in range(3):
                other = one if k == 0 else pltpu.roll(one, 8 - 2 * k, 0)
                near[k] = near[k] + weighted * other
        near = [n + pltpu.roll(n, 7, 0) for n in near]
        odd = (iota((8, 128), 0) & 1) == 1
        sp1[u, 0:8, :] = jnp.where(odd, pltpu.roll(near[1], 1, 0), near[0])
        sp1[u, 8:16, :] = near[2]

        @pl.when(u // 2 != place)
        def _():
            e_copy(u).start()

        @pl.when(u // 2 == place)
        def _():
            r1s[u % 2, place] = sp1[u]

    def g_copy(t, k):
        u = 2 * place + t
        return remote(sp2.at[t], r2s.at[column], g_send.at[t, k], g_recv.at[column],
                      device(u // 4, u % 4, k // 2, k % 2))

    def is_me(t, k):
        return jnp.logical_and(2 * place + t == column, k == place)

    def finish():
        for t in range(2):

            def add(k):
                @pl.when(k != place)
                def _():
                    remote(sp1.at[0], r1s.at[t, k], e_send.at[0], e_recv.at[t, k],
                           device(x, y, z, 1 - core)).wait_recv()

            loop(0, 8, add)
            total = r1s[t, 0]
            for k in range(1, 8):
                total = total + r1s[t, k]
            sp2[t] = total

            def send(k):
                @pl.when(jnp.logical_not(is_me(t, k)))
                def _():
                    g_copy(t, k).start()

                @pl.when(is_me(t, k))
                def _():
                    r2s[column] = sp2[t]

            loop(0, 8, send)

        def arrived(k):
            @pl.when(jnp.logical_not(jnp.logical_and(k == column, column // 2 == place)))
            def _():
                remote(sp2.at[0], r2s.at[k], g_send.at[0, 0], g_recv.at[k],
                       device(x, y, z, 1 - core)).wait_recv()

        loop(0, 16, arrived)
        total = r2s[0]
        for k in range(1, 16):
            total = total + r2s[k]
        ell = column * LANES + iota((16, 128), 1)
        total = total / (2 * ell + 1).astype(F32)
        share = ((z % 2) * 2 + core) * 2 + z // 2
        total = pltpu.roll(total, (128 - share * 16) % 128, 1)
        order = [0, 1, 8, 7, 2, 3, 10, 4, 5, 6]
        rows = jnp.concatenate([total[k : k + 1] for k in order], axis=0)
        spec_ref[...] = rows[:, 0:16]

    def orders():
        mine = perm[0, 384:400, :].astype(F32)
        m = jnp.sum(mine * iota((16, 512), 1).astype(F32), axis=1, keepdims=True)
        m = jnp.broadcast_to(m, (16, 128))
        full = jnp.concatenate(
            [jnp.broadcast_to(m[j : j + 1], (8, 128)) for j in range(4)], axis=0
        )
        morder[...] = full
        mweight[...] = jnp.where(full == 0.0, 1.0, 2.0)

    fourier()
    f_first().start()
    loop(0, PARTS, f_start)
    loop(0, 12, phase_a)
    orders()
    f_first().wait_recv()
    loop(0, PARTS, build)
    loop(0, 6, phase_b)
    loop(12, 16, phase_a)
    loop(6, 12, phase_b)
    loop(0, 6, phase_c)
    loop(12, 16, phase_b)
    loop(0, 6, phase_d)
    loop(6, 12, phase_c)
    loop(0, 6, phase_e)
    loop(6, 12, phase_d)
    loop(12, 16, phase_c)
    loop(6, 12, phase_e)
    loop(12, 16, phase_d)
    loop(12, 16, phase_e)
    finish()

    f_first().wait_send()

    def f_left(part):
        for copy in f_copies(part):
            copy.wait_send()

    loop(0, PARTS, f_left)

    def left(u):
        for copy in (*a_copies(u), b_copy(u), *c_copies(u), *d_copies(u)):
            copy.wait_send()

        @pl.when(u // 2 != place)
        def _():
            e_copy(u).wait_send()

    loop(0, UNITS, left)

    def g_left(k):
        for t in range(2):

            @pl.when(jnp.logical_not(is_me(t, k)))
            def _():
                g_copy(t, k).wait_send()

    loop(0, 8, g_left)


def per_device(sky_maps, legendre, owner_table, table, twiddle):
    vmem = pl.BlockSpec(memory_space=pltpu.VMEM)
    dma = pltpu.SemaphoreType.DMA
    V = pltpu.VMEM
    harm, spectra = pl.pallas_call(
        kernel,
        out_shape=(
            jax.ShapeDtypeStruct((32, 2048), F32),
            jax.ShapeDtypeStruct((10, 16), F32),
        ),
        in_specs=[vmem, pl.BlockSpec(memory_space=pl.ANY), vmem, vmem, vmem],
        out_specs=(vmem, vmem),
        scratch_shapes=[
            V((UNITS, 4, 512, 128), BF16),
            V((UNITS, 2, 4, 4, 64, 128), BF16),
            V((UNITS, 3, 2, 4, 64, 128), BF16),
            V((3, 512, 512), BF16),
            V((512, 512), BF16),
            V((PARTS, 8, 128, 256), BF16),
            V((512, 128), F32),
            V((512, 1024), F32),
            V((2, 16, 512), F32),
            V((32, 512), BF16),
            V((13, 32, 512), BF16),
            V((UNITS, 512, 128), F32),
            V((UNITS, 512, 128), BF16),
            V((UNITS, 512, 128), BF16),
            V((UNITS, 128, 128), F32),
            V((UNITS, 3, 128, 128), BF16),
            V((UNITS, 3, 128, 128), BF16),
            V((UNITS, 32, 128), F32),
            V((UNITS, 3, 32, 128), F32),
            V((UNITS, 3, 32, 128), F32),
            V((UNITS, 16, 128), F32),
            V((2, 8, 16, 128), F32),
            V((2, 16, 128), F32),
            V((16, 16, 128), F32),
            V((32, 128), F32),
            V((32, 128), F32),
            dma((UNITS,)),
            dma((UNITS, 3)), dma((UNITS, 3)),
            dma((13,)), dma((13,)),
            dma((UNITS,)), dma((UNITS,)),
            dma((UNITS, 3)), dma((UNITS, 3)),
            dma((UNITS, 3)), dma((UNITS, 3)),
            dma((UNITS,)), dma((2, 8)),
            dma((2, 8)), dma((16,)),
        ],
        compiler_params=pltpu.CompilerParams(
            has_side_effects=True, vmem_limit_bytes=60 * 1024 * 1024
        ),
        name="analysis",
    )(sky_maps, legendre, owner_table.reshape(1, 512), table, twiddle)
    return harm.reshape(4, 4, 2, 2048), spectra


def solution(mesh):
    both = ("blk", "grp")
    inner = jax.shard_map(
        per_device,
        mesh=mesh,
        in_specs=(P(None, both, None), P(both, None, None), P(), P(), P()),
        out_specs=(P(both, None, None, None), P(None, both)),
        check_vma=False,
    )

    def run(sky_maps, legendre, owner_table):
        table, twiddle = dft_tables()
        return inner(sky_maps, legendre, owner_table, jnp.asarray(table), jnp.asarray(twiddle))

    return run
```

profile of v0, /device:TPU:7, one launch (start us, length us, event | category | flops | bytes accessed | tf_op | source)
XLA Modules:
  0.0 86.6 jit_solution(10888833129086803913)
XLA Ops:
  0.6 82.9 %analysis.1 = (f32[32,2048]{1,0:T(8,128)}, f32[10,16]{1,0:T(8,128)}) custom-call(f32[4,4,4096]{2,1,0:T(4,128)} %sky_ref.1, bf16[4,512,2048]{2,1,0:T(8,128)(2,1)} %leg_ref.1, s32[1,512]{1,0:T(1,128)} %bitcast.1, f32[128,1024]{1,0:T(8,128)} %constant.4.clone.table_ref, f32[32,2,512]{2,1,0:T(2,128)} %constant.5.clone.twid_ref), custom_call_target="tpu_custom_call" | custom-call | tf_op jit(solution)/shard_map/analysis/pallas_call | solution.py:446
  83.5 1.8 %reshape.11 = f32[4,4,2,2048]{3,2,1,0:T(2,128)} reshape(f32[32,2048]{1,0:T(8,128)} %get-tuple-element.4) | data formatting | bytes 524288 | tf_op jit(solution)/shard_map/reshape | solution.py:495
  85.3 1.3 %copy.8 = f32[10,16]{1,0:T(8,128)} copy(f32[10,16]{1,0:T(8,128)} %get-tuple-element.9) | data formatting | bytes 1280
where the time goes:
time: 87.5 us; the launch traced here: 86.6 us
  Pallas kernels  82.9 us (95%)
  local copies, waits for them, and re-layouts  3.09 us (4%)
    pallas_call x1, Pallas kernels, per_device(): pl.pallas_call(kernel, out_shape=(jax.ShapeDtypeStruct((32, 2048), F32),...  82.9 us
    reshape x1, local copies, waits for them, and re-layouts, per_device(): return (harm.reshape(4, 4, 2, 2048), spectra)  1.8 us

commit v1 on v0

--- a/solution.py
+++ b/solution.py
@@ -33,11 +33,11 @@
 
 
 def kernel(
-    sky_ref, leg_ref, own_ref, table_ref, twid_ref, harm_ref, spec_ref,
-    legv, sendb, recvb, perm, hot, amat, fx, fz, fre, fown, frecv,
-    acc, passb, passr, acc2, s2, r2, acc3, s3, r3, sp1, r1s, sp2, r2s, morder, mweight,
-    leg_sem, a_send, a_recv, f_send, f_recv, b_send, b_recv, c_send, c_recv,
-    d_send, d_recv, e_send, e_recv, g_send, g_recv,
+    sky_in, leg_ref, own_ref, table_in, twid_in, harm_ref, spec_ref,
+    sky_ref, table_ref, twid_ref, legv, sendb, recvb, perm, hot, amat, fx, fz, fre, fown, frecv,
+    acc, passb, passr, acc2, s2, r2, acc3, s3, r3, sp, rsp, morder, mweight,
+    in_sem, leg_sem, a_send, a_recv, f_send, f_recv, b_send, b_recv, c_send, c_recv,
+    d_send, d_recv, e_send, e_recv,
 ):
     blk = lax.axis_index("blk")
     grp = lax.axis_index("grp")
@@ -81,11 +81,31 @@
 
         lax.fori_loop(lo, hi, body, 0)
 
+    barrier = pltpu.get_barrier_semaphore()
+    near_by = [device(x, y, z, 1 - core)]
+    for axis in range(3):
+        a1, a2, a3 = coords(axis)
+        for d in (1, 2, 3):
+            near_by.append(at(axis, (a1 + d) % 4, a2, a3, core))
+            if d != 2:
+                near_by.append(at(axis, (a1 + d) % 4, a2, a3, 1 - core))
+    for dev in near_by:
+        pl.semaphore_signal(barrier, inc=1, device_id=dev, device_id_type=MESH)
+
     def leg_copy(u):
         lanes = pl.ds(pl.multiple_of(u * LANES, LANES), LANES)
         return pltpu.make_async_copy(leg_ref.at[:, :, lanes], legv.at[u], leg_sem.at[u])
 
-    loop(0, UNITS, lambda u: leg_copy(u).start())
+    inputs = [
+        pltpu.make_async_copy(src, dst, in_sem.at[i])
+        for i, (src, dst) in enumerate(
+            [(sky_in, sky_ref), (table_in, table_ref), (twid_in, twid_ref)]
+        )
+    ]
+    loop(0, PARTS, lambda u: leg_copy(u).start())
+    for copy in inputs:
+        copy.start()
+    loop(PARTS, UNITS, lambda u: leg_copy(u).start())
 
     def hot_rows(i):
         rows = pl.ds(pl.multiple_of(i * 128, 128), 128)
@@ -143,6 +163,8 @@
             copy.start()
 
     def fourier():
+        for copy in inputs:
+            copy.wait()
         for a in range(4):
             for k1 in range(32):
                 fx[k1 * 16 + a * 4 : k1 * 16 + a * 4 + 4, :] = sky_ref[
@@ -285,24 +307,24 @@
             total = total + r2[u, d].astype(F32)
         acc3[u] = total[0:32]
         for d in range(3):
-            s3[u, d] = total[32 * d + 32 : 32 * d + 64]
+            s3[u, d] = total[32 * d + 32 : 32 * d + 64].astype(BF16)
         for copy in d_copies(u):
             copy.start()
 
-    column = x * 4 + y
-    place = z * 2 + core
-
-    def e_copy(u):
-        target = u // 2
-        return remote(sp1.at[u], r1s.at[u % 2, place], e_send.at[u], e_recv.at[u % 2, place],
-                      device(x, y, target // 2, target % 2))
+    me = blk * 2 + grp
+
+    def e_copy(u, k):
+        slot = (me - (u * 8 + k) + 255) % 128
+        return remote(sp.at[u, k], rsp.at[slot], e_send, e_recv, (u * 4 + k // 2, k % 2))
+
+    pair_rows = [(0, 0), (1, 0), (2, 0), (1, 6), (0, 2), (1, 2), (2, 2), (0, 4), (1, 4), (0, 6)]
 
     def phase_e(u):
         for copy in d_copies(u):
             copy.wait_recv()
         total = acc3[u]
         for d in range(3):
-            total = total + r3[u, d]
+            total = total + r3[u, d].astype(F32)
         ell = (u * LANES + iota((32, 128), 1)).astype(F32)
         total = jnp.where(ell >= morder[...], total, 0.0)
         harm_ref[:, pl.ds(pl.multiple_of(u * LANES, LANES), LANES)] = total
@@ -315,69 +337,41 @@
                 other = one if k == 0 else pltpu.roll(one, 8 - 2 * k, 0)
                 near[k] = near[k] + weighted * other
         near = [n + pltpu.roll(n, 7, 0) for n in near]
-        odd = (iota((8, 128), 0) & 1) == 1
-        sp1[u, 0:8, :] = jnp.where(odd, pltpu.roll(near[1], 1, 0), near[0])
-        sp1[u, 8:16, :] = near[2]
-
-        @pl.when(u // 2 != place)
-        def _():
-            e_copy(u).start()
-
-        @pl.when(u // 2 == place)
-        def _():
-            r1s[u % 2, place] = sp1[u]
-
-    def g_copy(t, k):
-        u = 2 * place + t
-        return remote(sp2.at[t], r2s.at[column], g_send.at[t, k], g_recv.at[column],
-                      device(u // 4, u % 4, k // 2, k % 2))
-
-    def is_me(t, k):
-        return jnp.logical_and(2 * place + t == column, k == place)
+        lane = iota((8, 128), 1) >> 4
+        packed = [jnp.zeros((8, 128), F32) for _ in range(2)]
+        for p, (k, row) in enumerate(pair_rows):
+            moved = near[k] if p % 8 == 0 else pltpu.roll(near[k], 16 * (p % 8), 1)
+            wide = jnp.broadcast_to(moved[row : row + 1], (8, 128))
+            wide = pltpu.roll(wide, 16, 1, stride=16, stride_axis=0)
+            packed[p // 8] = jnp.where(lane == p % 8, wide, packed[p // 8])
+        for k in range(8):
+            for half in range(2):
+                sp[u, k, half : half + 1, :] = packed[half][7 - k : 8 - k]
+
+        def send(k, c):
+            @pl.when(u * 8 + k != me)
+            def _():
+                e_copy(u, k).start()
+
+            return c
+
+        lax.fori_loop(0, 8, send, 0)
 
     def finish():
-        for t in range(2):
-
-            def add(k):
-                @pl.when(k != place)
-                def _():
-                    remote(sp1.at[0], r1s.at[t, k], e_send.at[0], e_recv.at[t, k],
-                           device(x, y, z, 1 - core)).wait_recv()
-
-            loop(0, 8, add)
-            total = r1s[t, 0]
-            for k in range(1, 8):
-                total = total + r1s[t, k]
-            sp2[t] = total
-
-            def send(k):
-                @pl.when(jnp.logical_not(is_me(t, k)))
-                def _():
-                    g_copy(t, k).start()
-
-                @pl.when(is_me(t, k))
-                def _():
-                    r2s[column] = sp2[t]
-
-            loop(0, 8, send)
-
-        def arrived(k):
-            @pl.when(jnp.logical_not(jnp.logical_and(k == column, column // 2 == place)))
-            def _():
-                remote(sp2.at[0], r2s.at[k], g_send.at[0, 0], g_recv.at[k],
-                       device(x, y, z, 1 - core)).wait_recv()
-
-        loop(0, 16, arrived)
-        total = r2s[0]
-        for k in range(1, 16):
-            total = total + r2s[k]
-        ell = column * LANES + iota((16, 128), 1)
-        total = total / (2 * ell + 1).astype(F32)
-        share = ((z % 2) * 2 + core) * 2 + z // 2
-        total = pltpu.roll(total, (128 - share * 16) % 128, 1)
-        order = [0, 1, 8, 7, 2, 3, 10, 4, 5, 6]
-        rows = jnp.concatenate([total[k : k + 1] for k in order], axis=0)
-        spec_ref[...] = rows[:, 0:16]
+        arrived = remote(rsp, rsp, e_send, e_recv, device(x, y, z, 1 - core))
+        arrived.wait_recv()
+        total = sp[me // 8, me % 8]
+        for k in range(127):
+            total = total + rsp[k]
+        rows = []
+        for half in range(2):
+            wide = jnp.broadcast_to(total[half : half + 1], (8, 128))
+            wide = pltpu.roll(wide, 16, 1, stride=16, stride_axis=0)
+            rows += [wide[7 - p : 8 - p, 0:16] for p in range(8)]
+        ell = me * 16 + iota((10, 16), 1)
+        power = jnp.concatenate(rows[0:10], axis=0)
+        spec_ref[...] = power / (2 * ell + 1).astype(F32)
+        arrived.wait_send()
 
     def orders():
         mine = perm[0, 384:400, :].astype(F32)
@@ -389,27 +383,37 @@
         morder[...] = full
         mweight[...] = jnp.where(full == 0.0, 1.0, 2.0)
 
-    fourier()
-    f_first().start()
-    loop(0, PARTS, f_start)
-    loop(0, 12, phase_a)
-    orders()
-    f_first().wait_recv()
-    loop(0, PARTS, build)
-    loop(0, 6, phase_b)
-    loop(12, 16, phase_a)
-    loop(6, 12, phase_b)
-    loop(0, 6, phase_c)
-    loop(12, 16, phase_b)
-    loop(0, 6, phase_d)
-    loop(6, 12, phase_c)
-    loop(0, 6, phase_e)
-    loop(6, 12, phase_d)
-    loop(12, 16, phase_c)
-    loop(6, 12, phase_e)
-    loop(12, 16, phase_d)
-    loop(12, 16, phase_e)
-    finish()
+    def phase(name, lo, hi, f):
+        with jax.named_scope(name):
+            loop(lo, hi, f)
+
+    with jax.named_scope("meet"):
+        pl.semaphore_wait(barrier, len(near_by))
+    phase("a0", 0, 6, phase_a)
+    with jax.named_scope("fourier"):
+        fourier()
+        f_first().start()
+        loop(0, PARTS, f_start)
+        orders()
+    phase("a1", 6, 12, phase_a)
+    with jax.named_scope("build"):
+        f_first().wait_recv()
+        loop(0, PARTS, build)
+    phase("b0", 0, 6, phase_b)
+    phase("a2", 12, 16, phase_a)
+    phase("b1", 6, 12, phase_b)
+    phase("c0", 0, 6, phase_c)
+    phase("b2", 12, 16, phase_b)
+    phase("d0", 0, 6, phase_d)
+    phase("c1", 6, 12, phase_c)
+    phase("e0", 0, 6, phase_e)
+    phase("d1", 6, 12, phase_d)
+    phase("c2", 12, 16, phase_c)
+    phase("e1", 6, 12, phase_e)
+    phase("d2", 12, 16, phase_d)
+    phase("e2", 12, 16, phase_e)
+    with jax.named_scope("finish"):
+        finish()
 
     f_first().wait_send()
 
@@ -423,24 +427,13 @@
         for copy in (*a_copies(u), b_copy(u), *c_copies(u), *d_copies(u)):
             copy.wait_send()
 
-        @pl.when(u // 2 != place)
-        def _():
-            e_copy(u).wait_send()
-
-    loop(0, UNITS, left)
-
-    def g_left(k):
-        for t in range(2):
-
-            @pl.when(jnp.logical_not(is_me(t, k)))
-            def _():
-                g_copy(t, k).wait_send()
-
-    loop(0, 8, g_left)
+    with jax.named_scope("left"):
+        loop(0, UNITS, left)
 
 
 def per_device(sky_maps, legendre, owner_table, table, twiddle):
     vmem = pl.BlockSpec(memory_space=pltpu.VMEM)
+    away = pl.BlockSpec(memory_space=pl.ANY)
     dma = pltpu.SemaphoreType.DMA
     V = pltpu.VMEM
     harm, spectra = pl.pallas_call(
@@ -449,9 +442,12 @@
             jax.ShapeDtypeStruct((32, 2048), F32),
             jax.ShapeDtypeStruct((10, 16), F32),
         ),
-        in_specs=[vmem, pl.BlockSpec(memory_space=pl.ANY), vmem, vmem, vmem],
+        in_specs=[away, away, vmem, away, away],
         out_specs=(vmem, vmem),
         scratch_shapes=[
+            V((4, 4, 4096), F32),
+            V((128, 1024), F32),
+            V((32, 2, 512), F32),
             V((UNITS, 4, 512, 128), BF16),
             V((UNITS, 2, 4, 4, 64, 128), BF16),
             V((UNITS, 3, 2, 4, 64, 128), BF16),
@@ -470,25 +466,22 @@
             V((UNITS, 3, 128, 128), BF16),
             V((UNITS, 3, 128, 128), BF16),
             V((UNITS, 32, 128), F32),
-            V((UNITS, 3, 32, 128), F32),
-            V((UNITS, 3, 32, 128), F32),
-            V((UNITS, 16, 128), F32),
-            V((2, 8, 16, 128), F32),
-            V((2, 16, 128), F32),
-            V((16, 16, 128), F32),
+            V((UNITS, 3, 32, 128), BF16),
+            V((UNITS, 3, 32, 128), BF16),
+            V((UNITS, 8, 2, 128), F32),
+            V((127, 2, 128), F32),
             V((32, 128), F32),
             V((32, 128), F32),
-            dma((UNITS,)),
+            dma((3,)), dma((UNITS,)),
             dma((UNITS, 3)), dma((UNITS, 3)),
             dma((13,)), dma((13,)),
             dma((UNITS,)), dma((UNITS,)),
             dma((UNITS, 3)), dma((UNITS, 3)),
             dma((UNITS, 3)), dma((UNITS, 3)),
-            dma((UNITS,)), dma((2, 8)),
-            dma((2, 8)), dma((16,)),
+            dma, dma,
         ],
         compiler_params=pltpu.CompilerParams(
-            has_side_effects=True, vmem_limit_bytes=60 * 1024 * 1024
+            collective_id=0, has_side_effects=True, vmem_limit_bytes=60 * 1024 * 1024
         ),
         name="analysis",
     )(sky_maps, legendre, owner_table.reshape(1, 512), table, twiddle)

time: 87.5 us -> 68.2 us (0.78)
  Pallas kernels: 82.9 us -> 64.2 us
    pallas_call x1, Pallas kernels: 82.9 us -> 64.2 us  [per_device(): pl.pallas_call(kernel, out_shape=(jax.ShapeDtypeStruct((32, 2048), F32),...]
where the time goes in v1:
time: 68.2 us; the launch traced here: 68 us
  Pallas kernels  64.2 us (94%)
  local copies, waits for them, and re-layouts  3.09 us (5%)
    pallas_call x1, Pallas kernels, per_device(): pl.pallas_call(kernel, out_shape=(jax.ShapeDtypeStruct((32, 2048), F32),...  64.2 us
    reshape x1, local copies, waits for them, and re-layouts, per_device(): return (harm.reshape(4, 4, 2, 2048), spectra)  1.8 us

profile of v1, /device:TPU:7, one launch (start us, length us, event | category | flops | bytes accessed | tf_op | source)
XLA Modules:
  0.0 68.0 jit_solution(16952118692950521216)
XLA Ops:
  0.6 64.2 %analysis.1 = (f32[32,2048]{1,0:T(8,128)}, f32[10,16]{1,0:T(8,128)}) custom-call(f32[4,4,4096]{2,1,0:T(4,128)} %sky_in.1, bf16[4,512,2048]{2,1,0:T(8,128)(2,1)} %leg_ref.1, s32[1,512]{1,0:T(1,128)} %bitcast.1, f32[128,1024]{1,0:T(8,128)} %constant.4.clone.table_in, f32[32,2,512]{2,1,0:T(2,128)} %constant.5.clone.twid_in), custom_call_target="tpu_custom_call" | custom-call | tf_op jit(solution)/shard_map/analysis/pallas_call | solution.py:439
  64.9 1.8 %reshape.11 = f32[4,4,2,2048]{3,2,1,0:T(2,128)} reshape(f32[32,2048]{1,0:T(8,128)} %get-tuple-element.4) | data formatting | bytes 524288 | tf_op jit(solution)/shard_map/reshape | solution.py:488
  66.7 1.3 %copy.8 = f32[10,16]{1,0:T(8,128)} copy(f32[10,16]{1,0:T(8,128)} %get-tuple-element.9) | data formatting | bytes 1280

commit v2 on v1

--- a/solution.py
+++ b/solution.py
@@ -29,15 +29,18 @@
     k1 = np.arange(32)[:, None]
     turn = 2.0 * math.pi * ((k1 * m) % 32) / 32.0
     twiddle = np.stack([np.cos(turn), np.sin(turn)], axis=1)
-    return table.astype(np.float32), twiddle.astype(np.float32)
+    table = table.astype(np.float32)
+    high = table.astype(jnp.bfloat16)
+    low = (table - high.astype(np.float32)).astype(jnp.bfloat16)
+    return np.concatenate([high, low], axis=0), twiddle.astype(np.float32)
 
 
 def kernel(
     sky_in, leg_ref, own_ref, table_in, twid_in, harm_ref, spec_ref,
-    sky_ref, table_ref, twid_ref, legv, sendb, recvb, perm, hot, amat, fx, fz, fre, fown, frecv,
-    acc, passb, passr, acc2, s2, r2, acc3, s3, r3, sp, rsp, morder, mweight,
-    in_sem, leg_sem, a_send, a_recv, f_send, f_recv, b_send, b_recv, c_send, c_recv,
-    d_send, d_recv, e_send, e_recv,
+    sky_ref, table_ref, twid_ref, legv, sendb, recvb, perm, hot, amat, spread, fx, fz, fre, fown, frecv,
+    acc, passb, passr, acc2, s2, r2, t2, q2, acc3, s3, r3, harm, sp, rsp, morder, mweight,
+    in_sem, leg_sem, out_sem, a_send, a_recv, f_send, f_recv, b_send, b_recv, c_send, c_recv,
+    h_send, h_recv, d_send, d_recv, e_send, e_recv,
 ):
     blk = lax.axis_index("blk")
     grp = lax.axis_index("grp")
@@ -116,38 +119,36 @@
 
     def perm_rows(axis):
         a1, a2, a3 = coords(axis)
-        step = 1 - 2 * (a1 % 2)
-        i = iota((512, 512), 0)
-        j = i & 3
+        i = iota((512, 128), 0)
         v3 = (a3 + (i >> 2)) & 3
-        v2 = (a2 + (i >> 4)) & 3
+        v2 = (a2 + ((i >> 4) + 1) * (1 - 2 * (a2 % 2)) + 128) & 3
+        v1 = (a1 + ((i >> 7) + 1) * (1 - 2 * (a1 % 2)) + 16) & 3
         cc = core ^ ((i >> 6) & 1)
-        v1 = (a1 + ((i >> 7) + 1) * step + 16) & 3
-        xx = pick(axis, v1, v3, v2)
-        yy = pick(axis, v2, v1, v3)
-        zz = pick(axis, v3, v2, v1)
-        slot = ((((xx * 4 + yy) * 2 + (zz & 1)) * 2 + cc) * 2 + (zz >> 1)) * 4 + j
-        chosen = jnp.where(slot == iota((512, 512), 1), 1.0, 0.0).astype(BF16)
+        xx, yy, zz = ((v1, v2, v3), (v3, v1, v2), (v2, v3, v1))[axis]
+        slot = (xx << 7) + (yy << 5) + ((zz & 1) << 4) + (cc << 3) + ((zz >> 1) << 2) + (i & 3)
+        slot = slot - iota((512, 128), 1)
+        chosen = jnp.concatenate(
+            [jnp.where(slot == k * 128, 1.0, 0.0).astype(BF16) for k in range(4)], axis=1
+        )
         rows = lax.dot_general(
             chosen, hot[...], (((1,), (1,)), ((), ())), preferred_element_type=F32
         )
         perm[axis] = rows.astype(BF16)
 
-    loop(0, 3, perm_rows)
-
     def a_copies(u):
         part, axis, par = part_of(u)
         a1, a2, a3, first, _ = pairs(axis, par)
+        sem = a_recv.at[u]
         return (
-            remote(sendb.at[u, 1, pl.ds(2, 2)], recvb.at[u, 0], a_send.at[u, 0], a_recv.at[u, 0],
+            remote(sendb.at[u, 0, pl.ds(0, 2)], recvb.at[u, 1], a_send, sem,
+                   at(axis, first, a2, a3, core)),
+            remote(sendb.at[u, 1, pl.ds(0, 2)], recvb.at[u, 2], a_send, sem,
+                   at(axis, first, a2, a3, 1 - core)),
+            remote(sendb.at[u, 1, pl.ds(2, 2)], recvb.at[u, 0], a_send, sem,
                    at(axis, a1, a2, a3, 1 - core)),
-            remote(sendb.at[u, 0, pl.ds(0, 2)], recvb.at[u, 1], a_send.at[u, 1], a_recv.at[u, 1],
-                   at(axis, first, a2, a3, core)),
-            remote(sendb.at[u, 1, pl.ds(0, 2)], recvb.at[u, 2], a_send.at[u, 2], a_recv.at[u, 2],
-                   at(axis, first, a2, a3, 1 - core)),
-        )
-
-    def phase_a(u):
+        )
+
+    def a_rows(u):
         part, axis, par = part_of(u)
         leg_copy(u).wait()
         roles = (3 * par, 1, 3 - 3 * par, 2)
@@ -159,8 +160,20 @@
                     piece = rows[rel * 128 + rc * 64 : rel * 128 + rc * 64 + 64]
                     sendb[u, rc, roles[rel], 2 * pair] = piece[:, :128]
                     sendb[u, rc, roles[rel], 2 * pair + 1] = piece[:, 128:]
+
+    def a_start(u):
         for copy in a_copies(u):
             copy.start()
+
+    def phase_a(u):
+        a_rows(u)
+        a_start(u)
+
+    def all_in(ref, sem):
+        remote(ref, ref, a_send, sem, device(x, y, z, 1 - core)).wait_recv()
+
+    def all_out(ref, sem):
+        remote(ref, ref, sem, e_recv, device(x, y, z, 1 - core)).wait_send()
 
     def fourier():
         for copy in inputs:
@@ -173,10 +186,14 @@
 
         def rows_of(i):
             rows = pl.ds(pl.multiple_of(i * 128, 128), 128)
+            pixels = fx[rows, :]
+            high = pixels.astype(BF16)
+            low = (pixels - high.astype(F32)).astype(BF16)
+            table = table_ref[0:128, :]
             fz[rows, :] = jnp.dot(
-                fx[rows, :], table_ref[...], precision=lax.Precision.HIGHEST,
+                jnp.concatenate([high, low], axis=1), jnp.concatenate([table, table], axis=0),
                 preferred_element_type=F32,
-            )
+            ) + jnp.dot(high, table_ref[128:256, :], preferred_element_type=F32)
 
         loop(0, 4, rows_of)
 
@@ -198,13 +215,13 @@
             fown[r * 8 : r * 8 + 8, :] = jnp.concatenate(rows, axis=0).astype(BF16)
 
     def f_first():
-        return remote(fown, frecv.at[0], f_send.at[0], f_recv.at[0], device(x, y, z, 1 - core))
+        return remote(fown, frecv.at[0], f_send, f_recv.at[6], device(x, y, z, 1 - core))
 
     def f_copies(part):
         a1, a2, a3, first, _ = pairs(part // 2, part % 2)
         return [
-            remote(fown, frecv.at[1 + 2 * part + k], f_send.at[1 + 2 * part + k],
-                   f_recv.at[1 + 2 * part + k], at(part // 2, first, a2, a3, core ^ k))
+            remote(fown, frecv.at[1 + 2 * part + k], f_send, f_recv.at[part],
+                   at(part // 2, first, a2, a3, core ^ k))
             for k in range(2)
         ]
 
@@ -214,8 +231,6 @@
 
     def build(part):
         axis, par = part // 2, part % 2
-        for copy in f_copies(part):
-            copy.wait_recv()
         four = jnp.concatenate(
             [fown[...], frecv[0], frecv[1 + 2 * part], frecv[2 + 2 * part]], axis=0
         )
@@ -224,10 +239,8 @@
         picked = lax.dot_general(
             four, mine, (((1,), (1,)), ((), ())), preferred_element_type=F32
         ).astype(BF16)
-        lane = iota((128, 1024), 1)
-        spread = (lane >> 7) * 16 + (lane & 15) == iota((128, 1024), 0)
         tiled = jnp.dot(
-            picked, jnp.where(spread, 1.0, 0.0).astype(BF16), preferred_element_type=F32
+            picked, spread[...], preferred_element_type=F32
         )
         group = iota((8, 128), 1) >> 4
         diagonal = (iota((128, 128), 0) >> 3) == (iota((128, 128), 1) & 15)
@@ -247,13 +260,12 @@
     def b_copy(u):
         part, axis, par = part_of(u)
         _, a2, a3, _, second = pairs(axis, par)
-        return remote(passb.at[u], passr.at[u], b_send.at[u], b_recv.at[u],
+        return remote(passb.at[u], passr.at[u], b_send, b_recv.at[u],
                       at(axis, second, a2, a3, core))
 
     def phase_b(u):
         part, axis, par = part_of(u)
-        for copy in a_copies(u):
-            copy.wait_recv()
+        all_in(recvb.at[u], a_recv.at[u])
         for g in range(8):
             sub, low = g // 4, 16 * (g % 4)
             slabs = [sendb[u, 0, 2 + sub, r, low : low + 16, :] for r in range(4)]
@@ -269,47 +281,57 @@
                 passb[u, rows, :] = out.astype(BF16)
         b_copy(u).start()
 
-    def c_copies(u):
+    def second_pairs(axis, par):
+        a1, a2, a3 = coords(axis)
+        step = (1 - 2 * (a2 % 2)) * (1 - 2 * par)
+        return (at(axis, a1, (a2 + step + 4) % 4, a3, core),
+                at(axis, a1, (a2 - step + 4) % 4, a3, core))
+
+    def c_copy(u):
+        part, axis, par = part_of(u)
+        return remote(s2.at[u], r2.at[u], c_send, c_recv.at[u], second_pairs(axis, par)[0])
+
+    def phase_c(u):
+        part, axis, par = part_of(u)
+        all_in(passr.at[u], b_recv.at[u])
+
+        def total(rel):
+            rows = pl.ds(pl.multiple_of(rel * 128, 128), 128)
+            return acc[u, rows, :] + passr[u, rows, :].astype(F32)
+
+        s2[u, 0] = total(2 * par).astype(BF16)
+        s2[u, 1] = total(1).astype(BF16)
+        c_copy(u).start()
+        acc2[u, 0] = total(3)
+        acc2[u, 1] = total(2 - 2 * par)
+
+    def h_copy(u):
+        part, axis, par = part_of(u)
+        return remote(t2.at[u], q2.at[u], h_send, h_recv.at[u], second_pairs(axis, par)[1])
+
+    def phase_h(u):
+        all_in(r2.at[u], c_recv.at[u])
+        t2[u] = (acc2[u, 1] + r2[u, 1].astype(F32)).astype(BF16)
+        h_copy(u).start()
+        acc2[u, 0] = acc2[u, 0] + r2[u, 0].astype(F32)
+
+    def d_copies(u):
         part, axis, par = part_of(u)
         a1, a2, a3 = coords(axis)
         return [
-            remote(s2.at[u, d], r2.at[u, d], c_send.at[u, d], c_recv.at[u, d],
-                   at(axis, a1, (a2 + d + 1) % 4, a3, core))
-            for d in range(3)
-        ]
-
-    def phase_c(u):
-        b_copy(u).wait_recv()
-        for d in range(4):
-            rows = slice(d * 128, d * 128 + 128)
-            total = acc[u, rows, :] + passr[u, rows, :].astype(F32)
-            if d == 0:
-                acc2[u] = total
-            else:
-                s2[u, d - 1] = total.astype(BF16)
-        for copy in c_copies(u):
-            copy.start()
-
-    def d_copies(u):
-        part, axis, par = part_of(u)
-        a1, a2, a3 = coords(axis)
-        return [
-            remote(s3.at[u, d], r3.at[u, d], d_send.at[u, d], d_recv.at[u, d],
+            remote(s3.at[u, d], r3.at[u, d], d_send, d_recv.at[u],
                    at(axis, a1, a2, (a3 + d + 1) % 4, core))
             for d in range(3)
         ]
 
     def phase_d(u):
-        for copy in c_copies(u):
-            copy.wait_recv()
-        total = acc2[u]
-        for d in range(3):
-            total = total + r2[u, d].astype(F32)
-        acc3[u] = total[0:32]
+        all_in(q2.at[u], h_recv.at[u])
+        total = acc2[u, 0] + q2[u].astype(F32)
         for d in range(3):
             s3[u, d] = total[32 * d + 32 : 32 * d + 64].astype(BF16)
         for copy in d_copies(u):
             copy.start()
+        acc3[u] = total[0:32]
 
     me = blk * 2 + grp
 
@@ -320,14 +342,15 @@
     pair_rows = [(0, 0), (1, 0), (2, 0), (1, 6), (0, 2), (1, 2), (2, 2), (0, 4), (1, 4), (0, 6)]
 
     def phase_e(u):
-        for copy in d_copies(u):
-            copy.wait_recv()
+        all_in(r3.at[u], d_recv.at[u])
         total = acc3[u]
         for d in range(3):
             total = total + r3[u, d].astype(F32)
         ell = (u * LANES + iota((32, 128), 1)).astype(F32)
         total = jnp.where(ell >= morder[...], total, 0.0)
-        harm_ref[:, pl.ds(pl.multiple_of(u * LANES, LANES), LANES)] = total
+        lanes = pl.ds(pl.multiple_of(u * LANES, LANES), LANES)
+        harm[:, lanes] = total
+        pltpu.make_async_copy(harm.at[:, lanes], harm_ref.at[:, lanes], out_sem).start()
         heavy = total * mweight[...]
         near = [jnp.zeros((8, 128), F32) for _ in range(3)]
         for j in range(4):
@@ -348,14 +371,11 @@
             for half in range(2):
                 sp[u, k, half : half + 1, :] = packed[half][7 - k : 8 - k]
 
-        def send(k, c):
+        for k in range(8):
+
             @pl.when(u * 8 + k != me)
             def _():
                 e_copy(u, k).start()
-
-            return c
-
-        lax.fori_loop(0, 8, send, 0)
 
     def finish():
         arrived = remote(rsp, rsp, e_send, e_recv, device(x, y, z, 1 - core))
@@ -372,9 +392,10 @@
         power = jnp.concatenate(rows[0:10], axis=0)
         spec_ref[...] = power / (2 * ell + 1).astype(F32)
         arrived.wait_send()
+        pltpu.make_async_copy(harm, harm_ref, out_sem).wait()
 
     def orders():
-        mine = perm[0, 384:400, :].astype(F32)
+        mine = perm[0, 432:448, :].astype(F32)
         m = jnp.sum(mine * iota((16, 512), 1).astype(F32), axis=1, keepdims=True)
         m = jnp.broadcast_to(m, (16, 128))
         full = jnp.concatenate(
@@ -387,48 +408,59 @@
         with jax.named_scope(name):
             loop(lo, hi, f)
 
-    with jax.named_scope("meet"):
-        pl.semaphore_wait(barrier, len(near_by))
-    phase("a0", 0, 6, phase_a)
+    with jax.named_scope("a0"):
+        perm_rows(0)
+        a_rows(0)
+        with jax.named_scope("meet"):
+            pl.semaphore_wait(barrier, len(near_by))
+        a_start(0)
+        perm_rows(1)
+        phase_a(2)
+        phase_a(1)
+        phase_a(3)
+        perm_rows(2)
+        loop(4, 6, phase_a)
     with jax.named_scope("fourier"):
         fourier()
         f_first().start()
         loop(0, PARTS, f_start)
+    phase("a1", 6, 12, phase_a)
+    phase("a2", 12, 16, phase_a)
+    with jax.named_scope("build"):
         orders()
-    phase("a1", 6, 12, phase_a)
-    with jax.named_scope("build"):
-        f_first().wait_recv()
-        loop(0, PARTS, build)
+        lane = iota((128, 1024), 1)
+        same = (lane >> 7) * 16 + (lane & 15) == iota((128, 1024), 0)
+        spread[...] = jnp.where(same, 1.0, 0.0).astype(BF16)
+        all_in(frecv.at[0], f_recv.at[6])
+        for part in range(PARTS):
+            all_in(frecv.at[pl.ds(1 + 2 * part, 2)], f_recv.at[part])
+        for part in range(PARTS):
+            build(part)
     phase("b0", 0, 6, phase_b)
-    phase("a2", 12, 16, phase_a)
     phase("b1", 6, 12, phase_b)
+    phase("b2", 12, 16, phase_b)
     phase("c0", 0, 6, phase_c)
-    phase("b2", 12, 16, phase_b)
+    phase("c1", 6, 12, phase_c)
+    phase("c2", 12, 16, phase_c)
+    phase("h0", 0, 6, phase_h)
+    phase("h1", 6, 12, phase_h)
+    phase("h2", 12, 16, phase_h)
     phase("d0", 0, 6, phase_d)
-    phase("c1", 6, 12, phase_c)
+    phase("d1", 6, 12, phase_d)
+    phase("d2", 12, 16, phase_d)
     phase("e0", 0, 6, phase_e)
-    phase("d1", 6, 12, phase_d)
-    phase("c2", 12, 16, phase_c)
     phase("e1", 6, 12, phase_e)
-    phase("d2", 12, 16, phase_d)
     phase("e2", 12, 16, phase_e)
     with jax.named_scope("finish"):
         finish()
 
-    f_first().wait_send()
-
-    def f_left(part):
-        for copy in f_copies(part):
-            copy.wait_send()
-
-    loop(0, PARTS, f_left)
-
-    def left(u):
-        for copy in (*a_copies(u), b_copy(u), *c_copies(u), *d_copies(u)):
-            copy.wait_send()
-
     with jax.named_scope("left"):
-        loop(0, UNITS, left)
+        all_out(frecv, f_send)
+        all_out(recvb, a_send)
+        all_out(passb, b_send)
+        all_out(s2, c_send)
+        all_out(t2, h_send)
+        all_out(s3, d_send)
 
 
 def per_device(sky_maps, legendre, owner_table, table, twiddle):
@@ -443,10 +475,10 @@
             jax.ShapeDtypeStruct((10, 16), F32),
         ),
         in_specs=[away, away, vmem, away, away],
-        out_specs=(vmem, vmem),
+        out_specs=(away, vmem),
         scratch_shapes=[
             V((4, 4, 4096), F32),
-            V((128, 1024), F32),
+            V((256, 1024), BF16),
             V((32, 2, 512), F32),
             V((UNITS, 4, 512, 128), BF16),
             V((UNITS, 2, 4, 4, 64, 128), BF16),
@@ -454,6 +486,7 @@
             V((3, 512, 512), BF16),
             V((512, 512), BF16),
             V((PARTS, 8, 128, 256), BF16),
+            V((128, 1024), BF16),
             V((512, 128), F32),
             V((512, 1024), F32),
             V((2, 16, 512), F32),
@@ -462,22 +495,22 @@
             V((UNITS, 512, 128), F32),
             V((UNITS, 512, 128), BF16),
             V((UNITS, 512, 128), BF16),
-            V((UNITS, 128, 128), F32),
-            V((UNITS, 3, 128, 128), BF16),
-            V((UNITS, 3, 128, 128), BF16),
+            V((UNITS, 2, 128, 128), F32),
+            V((UNITS, 2, 128, 128), BF16),
+            V((UNITS, 2, 128, 128), BF16),
+            V((UNITS, 128, 128), BF16),
+            V((UNITS, 128, 128), BF16),
             V((UNITS, 32, 128), F32),
             V((UNITS, 3, 32, 128), BF16),
             V((UNITS, 3, 32, 128), BF16),
+            V((32, 2048), F32),
             V((UNITS, 8, 2, 128), F32),
             V((127, 2, 128), F32),
             V((32, 128), F32),
             V((32, 128), F32),
-            dma((3,)), dma((UNITS,)),
-            dma((UNITS, 3)), dma((UNITS, 3)),
-            dma((13,)), dma((13,)),
-            dma((UNITS,)), dma((UNITS,)),
-            dma((UNITS, 3)), dma((UNITS, 3)),
-            dma((UNITS, 3)), dma((UNITS, 3)),
+            dma((3,)), dma((UNITS,)), dma,
+            dma, dma((UNITS,)), dma, dma((7,)),
+            dma, dma((UNITS,)), dma, dma((UNITS,)), dma, dma((UNITS,)), dma, dma((UNITS,)),
             dma, dma,
         ],
         compiler_params=pltpu.CompilerParams(

time: 68.2 us -> 60.4 us (0.89)
  Pallas kernels: 64.2 us -> 56.4 us
    pallas_call x1, Pallas kernels: 64.2 us -> 56.4 us  [per_device(): pl.pallas_call(kernel, out_shape=(jax.ShapeDtypeStruct((32, 2048), F32),...]
where the time goes in v2:
time: 60.4 us; the launch traced here: 60.1 us
  Pallas kernels  56.4 us (93%)
  local copies, waits for them, and re-layouts  3.09 us (5%)
  between operations  0.64 us (1%)
    pallas_call x1, Pallas kernels, per_device(): pl.pallas_call(kernel, out_shape=(jax.ShapeDtypeStruct((32, 2048), F32),...  56.4 us
    reshape x1, local copies, waits for them, and re-layouts, per_device(): return (harm.reshape(4, 4, 2, 2048), spectra)  1.8 us
    unnamed x1, local copies, waits for them, and re-layouts  1.29 us

profile of v2, /device:TPU:7, one launch (start us, length us, event | category | flops | bytes accessed | tf_op | source)
XLA Modules:
  0.0 60.1 jit_solution(18081652711266370707)
XLA Ops:
  0.6 56.4 %analysis.1 = (f32[32,2048]{1,0:T(8,128)}, f32[10,16]{1,0:T(8,128)}) custom-call(f32[4,4,4096]{2,1,0:T(4,128)} %sky_in.1, bf16[4,512,2048]{2,1,0:T(8,128)(2,1)} %leg_ref.1, s32[1,512]{1,0:T(1,128)} %bitcast.1, bf16[256,1024]{1,0:T(8,128)(2,1)} %constant.4.clone.table_in, f32[32,2,512]{2,1,0:T(2,128)} %constant.5.clone.twid_in), custom_call_target="tpu_custom_call" | custom-call | tf_op jit(solution)/shard_map/analysis/pallas_call | solution.py:471
  57.1 1.8 %reshape.11 = f32[4,4,2,2048]{3,2,1,0:T(2,128)} reshape(f32[32,2048]{1,0:T(8,128)} %get-tuple-element.4) | data formatting | bytes 524288 | tf_op jit(solution)/shard_map/reshape | solution.py:521
  58.9 1.3 %copy.8 = f32[10,16]{1,0:T(8,128)} copy(f32[10,16]{1,0:T(8,128)} %get-tuple-element.9) | data formatting | bytes 1280

commit v3 on v2

--- a/solution.py
+++ b/solution.py
@@ -32,14 +32,18 @@
     table = table.astype(np.float32)
     high = table.astype(jnp.bfloat16)
     low = (table - high.astype(np.float32)).astype(jnp.bfloat16)
-    return np.concatenate([high, low], axis=0), twiddle.astype(np.float32)
+    lane = np.arange(1024)[None, :]
+    spread = (lane >> 7) * 16 + (lane & 15) == np.arange(128)[:, None]
+    diagonal = (np.arange(128)[:, None] >> 3) == (np.arange(128)[None, :] & 15)
+    small = np.concatenate([spread, np.tile(diagonal, (1, 8))], axis=0).astype(jnp.bfloat16)
+    return np.concatenate([high, low, small], axis=0), twiddle.astype(np.float32)
 
 
 def kernel(
-    sky_in, leg_ref, own_ref, table_in, twid_in, harm_ref, spec_ref,
-    sky_ref, table_ref, twid_ref, legv, sendb, recvb, perm, hot, amat, spread, fx, fz, fre, fown, frecv,
-    acc, passb, passr, acc2, s2, r2, t2, q2, acc3, s3, r3, harm, sp, rsp, morder, mweight,
-    in_sem, leg_sem, out_sem, a_send, a_recv, f_send, f_recv, b_send, b_recv, c_send, c_recv,
+    sky_in, leg_ref, own_in, table_in, twid_in, harm_ref, spec_ref,
+    sky_ref, own_ref, table_ref, twid_ref, legv, sendb, recvb, perm, hot, amat, fx, fz, fre, fown, fkeep, fsend, frecv,
+    acc, passb, passr, acc2, s2, r2, t2, q2, acc3, s3, r3, sp, rsp, morder, mweight,
+    in_sem, leg_sem, a_send, a_recv, f_send, f_recv, b_send, b_recv, c_send, c_recv,
     h_send, h_recv, d_send, d_recv, e_send, e_recv,
 ):
     blk = lax.axis_index("blk")
@@ -102,13 +106,15 @@
     inputs = [
         pltpu.make_async_copy(src, dst, in_sem.at[i])
         for i, (src, dst) in enumerate(
-            [(sky_in, sky_ref), (table_in, table_ref), (twid_in, twid_ref)]
+            [(own_in, own_ref), (sky_in, sky_ref), (table_in, table_ref), (twid_in, twid_ref)]
         )
     ]
+    inputs[0].start()
     loop(0, PARTS, lambda u: leg_copy(u).start())
-    for copy in inputs:
+    for copy in inputs[1:]:
         copy.start()
     loop(PARTS, UNITS, lambda u: leg_copy(u).start())
+    inputs[0].wait()
 
     def hot_rows(i):
         rows = pl.ds(pl.multiple_of(i * 128, 128), 128)
@@ -120,7 +126,7 @@
     def perm_rows(axis):
         a1, a2, a3 = coords(axis)
         i = iota((512, 128), 0)
-        v3 = (a3 + (i >> 2)) & 3
+        v3 = (a3 + ((i >> 2) + 1) * (1 - 2 * (a3 % 2)) + 512) & 3
         v2 = (a2 + ((i >> 4) + 1) * (1 - 2 * (a2 % 2)) + 128) & 3
         v1 = (a1 + ((i >> 7) + 1) * (1 - 2 * (a1 % 2)) + 16) & 3
         cc = core ^ ((i >> 6) & 1)
@@ -176,7 +182,7 @@
         remote(ref, ref, sem, e_recv, device(x, y, z, 1 - core)).wait_send()
 
     def fourier():
-        for copy in inputs:
+        for copy in inputs[1:]:
             copy.wait()
         for a in range(4):
             for k1 in range(32):
@@ -214,48 +220,60 @@
             rows = [fre[q, a * 4 + r : a * 4 + r + 1, :] for a in range(4) for q in range(2)]
             fown[r * 8 : r * 8 + 8, :] = jnp.concatenate(rows, axis=0).astype(BF16)
 
-    def f_first():
-        return remote(fown, frecv.at[0], f_send, f_recv.at[6], device(x, y, z, 1 - core))
-
     def f_copies(part):
-        a1, a2, a3, first, _ = pairs(part // 2, part % 2)
-        return [
-            remote(fown, frecv.at[1 + 2 * part + k], f_send, f_recv.at[part],
-                   at(part // 2, first, a2, a3, core ^ k))
-            for k in range(2)
-        ]
-
-    def f_start(part):
-        for copy in f_copies(part):
-            copy.start()
+        axis, par = part // 2, part % 2
+        a1, a2, a3, first, _ = pairs(axis, par)
+        sem = f_recv.at[part]
+        return (
+            remote(fsend.at[part, 0], frecv.at[part, 1], f_send, sem, at(axis, first, a2, a3, core)),
+            remote(fsend.at[part, 1], frecv.at[part, 2], f_send, sem,
+                   at(axis, first, a2, a3, 1 - core)),
+            remote(fsend.at[part, 2], frecv.at[part, 0], f_send, sem,
+                   at(axis, a1, a2, a3, 1 - core)),
+        )
+
+    def f_start():
+        low = iota((32, 128), 1) < 64
+        for axis in range(3):
+            cols = lax.dot_general(
+                fown[...], perm[axis], (((1,), (1,)), ((), ())), preferred_element_type=F32
+            )
+            tile = [cols[:, k * 128 : k * 128 + 128] for k in range(4)]
+            turned = [pltpu.roll(t, 64, 1) for t in tile]
+
+            def joined(mine, passed, rc):
+                if rc == 0:
+                    return jnp.where(low, tile[mine], turned[passed]).astype(BF16)
+                return jnp.where(low, turned[mine], tile[passed]).astype(BF16)
+
+            for par in range(2):
+                part = 2 * axis + par
+                fsend[part, 0] = joined(2 * par, 1, 0)
+                fsend[part, 1] = joined(2 * par, 1, 1)
+                fsend[part, 2] = joined(3, 2 - 2 * par, 1)
+                fkeep[part] = joined(3, 2 - 2 * par, 0)
+                for copy in f_copies(part):
+                    copy.start()
 
     def build(part):
-        axis, par = part // 2, part % 2
-        four = jnp.concatenate(
-            [fown[...], frecv[0], frecv[1 + 2 * part], frecv[2 + 2 * part]], axis=0
-        )
-        passed = pl.multiple_of((2 - 2 * par) * 128, 128)
-        mine = jnp.concatenate([perm[axis, 384:448, :], perm[axis, pl.ds(passed, 64), :]], axis=0)
-        picked = lax.dot_general(
-            four, mine, (((1,), (1,)), ((), ())), preferred_element_type=F32
-        ).astype(BF16)
-        tiled = jnp.dot(
-            picked, spread[...], preferred_element_type=F32
-        )
+        all_in(frecv.at[part], f_recv.at[part])
+        picked = jnp.concatenate([fkeep[part]] + [frecv[part, k] for k in range(3)], axis=0)
+        tiled = jnp.dot(picked, table_ref[256:384, :], preferred_element_type=F32)
         group = iota((8, 128), 1) >> 4
-        diagonal = (iota((128, 128), 0) >> 3) == (iota((128, 128), 1) & 15)
         for g in range(8):
             for h in range(2):
-                base = jnp.zeros((8, 128), F32)
-                for i in range(8):
+                base = tiled[64 * h : 64 * h + 8, g * 128 : g * 128 + 128]
+                for i in range(1, 8):
                     row = (8 * h + i) * 8
                     base = jnp.where(
                         group == i, tiled[row : row + 8, g * 128 : g * 128 + 128], base
                     )
-                full = jnp.concatenate([base] * 16, axis=0)
-                amat[part, g, :, h * 128 : h * 128 + 128] = jnp.where(diagonal, full, 0.0).astype(
-                    BF16
-                )
+                two = jnp.concatenate([base, base], axis=0).astype(BF16)
+                for k in range(8):
+                    rows = slice(16 * k, 16 * k + 16)
+                    amat[part, g, rows, h * 128 : h * 128 + 128] = (
+                        two * table_ref[384 + 16 * k : 400 + 16 * k, 0:128]
+                    )
 
     def b_copy(u):
         part, axis, par = part_of(u)
@@ -281,33 +299,55 @@
                 passb[u, rows, :] = out.astype(BF16)
         b_copy(u).start()
 
-    def second_pairs(axis, par):
+    def second_axis(u):
+        part, axis, par = part_of(u)
+        late = u >= 12
+        return jnp.where(axis == 0, jnp.where(late, 0, 1), jnp.where(axis == 1, jnp.where(late, 1, 0), par))
+
+    def to_second(u, v, sign):
+        part, axis, par = part_of(u)
         a1, a2, a3 = coords(axis)
-        step = (1 - 2 * (a2 % 2)) * (1 - 2 * par)
-        return (at(axis, a1, (a2 + step + 4) % 4, a3, core),
-                at(axis, a1, (a2 - step + 4) % 4, a3, core))
+        swap = second_axis(u)
+        old = jnp.where(swap == 0, a2, a3)
+        new = (old + sign * v * (1 - 2 * (old % 2)) + 16) % 4
+        return at(axis, a1, jnp.where(swap == 0, new, a2), jnp.where(swap == 0, a3, new), core)
+
+    def to_third(u, v):
+        part, axis, par = part_of(u)
+        a1, a2, a3 = coords(axis)
+        swap = second_axis(u)
+        old = jnp.where(swap == 0, a3, a2)
+        new = (old + v * (1 - 2 * (old % 2)) + 16) % 4
+        return at(axis, a1, jnp.where(swap == 0, a2, new), jnp.where(swap == 0, new, a3), core)
+
+    def turn(u):
+        return (u + u // PARTS) % 2
 
     def c_copy(u):
-        part, axis, par = part_of(u)
-        return remote(s2.at[u], r2.at[u], c_send, c_recv.at[u], second_pairs(axis, par)[0])
+        return remote(s2.at[u], r2.at[u], c_send, c_recv.at[u], to_second(u, 1, 1 - 2 * turn(u)))
 
     def phase_c(u):
-        part, axis, par = part_of(u)
+        swap = second_axis(u)
+        par = turn(u)
         all_in(passr.at[u], b_recv.at[u])
 
-        def total(rel):
-            rows = pl.ds(pl.multiple_of(rel * 128, 128), 128)
+        def total(second, third):
+            start = second * jnp.where(swap == 0, 128, 32) + third * jnp.where(swap == 0, 32, 128)
+            rows = pl.ds(pl.multiple_of(start, 32), 32)
             return acc[u, rows, :] + passr[u, rows, :].astype(F32)
 
-        s2[u, 0] = total(2 * par).astype(BF16)
-        s2[u, 1] = total(1).astype(BF16)
+        for third in range(4):
+            rows = slice(32 * third, 32 * third + 32)
+            s2[u, 0, rows] = total(2 * par, third).astype(BF16)
+            s2[u, 1, rows] = total(1, third).astype(BF16)
         c_copy(u).start()
-        acc2[u, 0] = total(3)
-        acc2[u, 1] = total(2 - 2 * par)
+        for third in range(4):
+            rows = slice(32 * third, 32 * third + 32)
+            acc2[u, 0, rows] = total(3, third)
+            acc2[u, 1, rows] = total(2 - 2 * par, third)
 
     def h_copy(u):
-        part, axis, par = part_of(u)
-        return remote(t2.at[u], q2.at[u], h_send, h_recv.at[u], second_pairs(axis, par)[1])
+        return remote(t2.at[u], q2.at[u], h_send, h_recv.at[u], to_second(u, 1, 2 * turn(u) - 1))
 
     def phase_h(u):
         all_in(r2.at[u], c_recv.at[u])
@@ -316,11 +356,8 @@
         acc2[u, 0] = acc2[u, 0] + r2[u, 0].astype(F32)
 
     def d_copies(u):
-        part, axis, par = part_of(u)
-        a1, a2, a3 = coords(axis)
         return [
-            remote(s3.at[u, d], r3.at[u, d], d_send, d_recv.at[u],
-                   at(axis, a1, a2, (a3 + d + 1) % 4, core))
+            remote(s3.at[u, d], r3.at[u, d], d_send, d_recv.at[u], to_third(u, d + 1))
             for d in range(3)
         ]
 
@@ -328,10 +365,10 @@
         all_in(q2.at[u], h_recv.at[u])
         total = acc2[u, 0] + q2[u].astype(F32)
         for d in range(3):
-            s3[u, d] = total[32 * d + 32 : 32 * d + 64].astype(BF16)
+            s3[u, d] = total[32 * d : 32 * d + 32].astype(BF16)
         for copy in d_copies(u):
             copy.start()
-        acc3[u] = total[0:32]
+        acc3[u] = total[96:128]
 
     me = blk * 2 + grp
 
@@ -349,8 +386,7 @@
         ell = (u * LANES + iota((32, 128), 1)).astype(F32)
         total = jnp.where(ell >= morder[...], total, 0.0)
         lanes = pl.ds(pl.multiple_of(u * LANES, LANES), LANES)
-        harm[:, lanes] = total
-        pltpu.make_async_copy(harm.at[:, lanes], harm_ref.at[:, lanes], out_sem).start()
+        harm_ref[:, lanes] = total
         heavy = total * mweight[...]
         near = [jnp.zeros((8, 128), F32) for _ in range(3)]
         for j in range(4):
@@ -380,9 +416,10 @@
     def finish():
         arrived = remote(rsp, rsp, e_send, e_recv, device(x, y, z, 1 - core))
         arrived.wait_recv()
-        total = sp[me // 8, me % 8]
-        for k in range(127):
-            total = total + rsp[k]
+        sums = [sp[me // 8, me % 8], rsp[124], rsp[125], rsp[126]]
+        for k in range(124):
+            sums[k % 4] = sums[k % 4] + rsp[k]
+        total = (sums[0] + sums[1]) + (sums[2] + sums[3])
         rows = []
         for half in range(2):
             wide = jnp.broadcast_to(total[half : half + 1], (8, 128))
@@ -392,14 +429,13 @@
         power = jnp.concatenate(rows[0:10], axis=0)
         spec_ref[...] = power / (2 * ell + 1).astype(F32)
         arrived.wait_send()
-        pltpu.make_async_copy(harm, harm_ref, out_sem).wait()
 
     def orders():
         mine = perm[0, 432:448, :].astype(F32)
         m = jnp.sum(mine * iota((16, 512), 1).astype(F32), axis=1, keepdims=True)
         m = jnp.broadcast_to(m, (16, 128))
         full = jnp.concatenate(
-            [jnp.broadcast_to(m[j : j + 1], (8, 128)) for j in range(4)], axis=0
+            [jnp.broadcast_to(m[j : j + 1], (8, 128)) for j in range(12, 16)], axis=0
         )
         morder[...] = full
         mweight[...] = jnp.where(full == 0.0, 1.0, 2.0)
@@ -422,34 +458,35 @@
         loop(4, 6, phase_a)
     with jax.named_scope("fourier"):
         fourier()
-        f_first().start()
-        loop(0, PARTS, f_start)
+        f_start()
     phase("a1", 6, 12, phase_a)
-    phase("a2", 12, 16, phase_a)
     with jax.named_scope("build"):
-        orders()
-        lane = iota((128, 1024), 1)
-        same = (lane >> 7) * 16 + (lane & 15) == iota((128, 1024), 0)
-        spread[...] = jnp.where(same, 1.0, 0.0).astype(BF16)
-        all_in(frecv.at[0], f_recv.at[6])
-        for part in range(PARTS):
-            all_in(frecv.at[pl.ds(1 + 2 * part, 2)], f_recv.at[part])
         for part in range(PARTS):
             build(part)
-    phase("b0", 0, 6, phase_b)
-    phase("b1", 6, 12, phase_b)
-    phase("b2", 12, 16, phase_b)
-    phase("c0", 0, 6, phase_c)
-    phase("c1", 6, 12, phase_c)
-    phase("c2", 12, 16, phase_c)
-    phase("h0", 0, 6, phase_h)
-    phase("h1", 6, 12, phase_h)
-    phase("h2", 12, 16, phase_h)
-    phase("d0", 0, 6, phase_d)
-    phase("d1", 6, 12, phase_d)
-    phase("d2", 12, 16, phase_d)
-    phase("e0", 0, 6, phase_e)
-    phase("e1", 6, 12, phase_e)
+    phase("bX0", 0, 6, phase_b)
+    phase("aX2", 12, 16, phase_a)
+    phase("bZ1", 10, 12, phase_b)
+    phase("bX1", 6, 10, phase_b)
+    with jax.named_scope("orders"):
+        orders()
+    phase("cX0", 0, 4, phase_c)
+    phase("bX2", 12, 16, phase_b)
+    phase("cZ0", 4, 6, phase_c)
+    phase("cZ1", 10, 12, phase_c)
+    phase("hX0", 0, 4, phase_h)
+    phase("cX1", 6, 10, phase_c)
+    phase("cX2", 12, 16, phase_c)
+    phase("hX1", 6, 10, phase_h)
+    phase("hZ0", 4, 6, phase_h)
+    phase("hZ1", 10, 12, phase_h)
+    phase("dX0", 0, 4, phase_d)
+    phase("hX2", 12, 16, phase_h)
+    phase("dX1", 6, 10, phase_d)
+    phase("dZ0", 4, 6, phase_d)
+    phase("dZ1", 10, 12, phase_d)
+    phase("eX0", 0, 4, phase_e)
+    phase("dX2", 12, 16, phase_d)
+    phase("e1", 4, 12, phase_e)
     phase("e2", 12, 16, phase_e)
     with jax.named_scope("finish"):
         finish()
@@ -465,20 +502,22 @@
 
 def per_device(sky_maps, legendre, owner_table, table, twiddle):
     vmem = pl.BlockSpec(memory_space=pltpu.VMEM)
-    away = pl.BlockSpec(memory_space=pl.ANY)
+    away = pl.BlockSpec(memory_space=pltpu.HBM)
     dma = pltpu.SemaphoreType.DMA
     V = pltpu.VMEM
+    inputs = (sky_maps, legendre, owner_table.reshape(1, 512), table, twiddle)
     harm, spectra = pl.pallas_call(
         kernel,
         out_shape=(
             jax.ShapeDtypeStruct((32, 2048), F32),
             jax.ShapeDtypeStruct((10, 16), F32),
         ),
-        in_specs=[away, away, vmem, away, away],
-        out_specs=(away, vmem),
+        in_specs=[away] * 5,
+        out_specs=(vmem, vmem),
         scratch_shapes=[
             V((4, 4, 4096), F32),
-            V((256, 1024), BF16),
+            V((1, 512), jnp.int32),
+            V((512, 1024), BF16),
             V((32, 2, 512), F32),
             V((UNITS, 4, 512, 128), BF16),
             V((UNITS, 2, 4, 4, 64, 128), BF16),
@@ -486,12 +525,13 @@
             V((3, 512, 512), BF16),
             V((512, 512), BF16),
             V((PARTS, 8, 128, 256), BF16),
-            V((128, 1024), BF16),
             V((512, 128), F32),
             V((512, 1024), F32),
             V((2, 16, 512), F32),
             V((32, 512), BF16),
-            V((13, 32, 512), BF16),
+            V((PARTS, 32, 128), BF16),
+            V((PARTS, 3, 32, 128), BF16),
+            V((PARTS, 3, 32, 128), BF16),
             V((UNITS, 512, 128), F32),
             V((UNITS, 512, 128), BF16),
             V((UNITS, 512, 128), BF16),
@@ -503,21 +543,20 @@
             V((UNITS, 32, 128), F32),
             V((UNITS, 3, 32, 128), BF16),
             V((UNITS, 3, 32, 128), BF16),
-            V((32, 2048), F32),
             V((UNITS, 8, 2, 128), F32),
             V((127, 2, 128), F32),
             V((32, 128), F32),
             V((32, 128), F32),
-            dma((3,)), dma((UNITS,)), dma,
-            dma, dma((UNITS,)), dma, dma((7,)),
+            dma((4,)), dma((UNITS,)),
+            dma, dma((UNITS,)), dma, dma((PARTS,)),
             dma, dma((UNITS,)), dma, dma((UNITS,)), dma, dma((UNITS,)), dma, dma((UNITS,)),
             dma, dma,
         ],
         compiler_params=pltpu.CompilerParams(
-            collective_id=0, has_side_effects=True, vmem_limit_bytes=60 * 1024 * 1024
+            collective_id=0, has_side_effects=True, vmem_limit_bytes=50 * 1024 * 1024
         ),
         name="analysis",
-    )(sky_maps, legendre, owner_table.reshape(1, 512), table, twiddle)
+    )(*[pltpu.with_memory_space_constraint(v, pltpu.HBM) for v in inputs])
     return harm.reshape(4, 4, 2, 2048), spectra
 
 

time: 60.4 us -> 56.4 us (0.934)
  Pallas kernels: 56.4 us -> 54.2 us
  local copies, waits for them, and re-layouts: 3.09 us -> 1.45 us
    pallas_call x1, Pallas kernels: 56.4 us -> 54.2 us  [per_device(): pl.pallas_call(kernel, out_shape=(jax.ShapeDtypeStruct((32, 2048), F32),...]
    reshape x1, local copies, waits for them, and re-layouts: 1.8 us -> 0.85 us  [per_device(): return (harm.reshape(4, 4, 2, 2048), spectra)]
    unnamed x1, local copies, waits for them, and re-layouts: 1.29 us -> 0.6 us
where the time goes in v3:
time: 56.4 us; the launch traced here: 56.2 us
  Pallas kernels  54.2 us (96%)
  local copies, waits for them, and re-layouts  1.45 us (3%)
  between operations  0.64 us (1%)
    pallas_call x1, Pallas kernels, per_device(): pl.pallas_call(kernel, out_shape=(jax.ShapeDtypeStruct((32, 2048), F32),...  54.2 us

profile of v3, /device:TPU:7, one launch (start us, length us, event | category | flops | bytes accessed | tf_op | source)
XLA Modules:
  0.0 56.2 jit_solution(14947187862564215223)
XLA Ops:
  0.6 54.2 %analysis.1 = (f32[32,2048]{1,0:T(8,128)S(1)}, f32[10,16]{1,0:T(8,128)S(1)}) custom-call(f32[4,4,4096]{2,1,0:T(4,128)} %sky_in.1, bf16[4,512,2048]{2,1,0:T(8,128)(2,1)} %leg_ref.1, s32[1,512]{1,0:T(1,128)} %bitcast.1, bf16[512,1024]{1,0:T(8,128)(2,1)} %constant.4.clone.table_in, f32[32,2,512]{2,1,0:T(2,128)} %constant.5.clone.twid_in), custom_call_target="tpu_custom_call" | custom-call | tf_op jit(solution)/shard_map/analysis/pallas_call | solution.py:509
  54.8 0.8 %reshape.11 = f32[4,4,2,2048]{3,2,1,0:T(2,128)} reshape(f32[32,2048]{1,0:T(8,128)S(1)} %get-tuple-element.4) | data formatting | bytes 524288 | tf_op jit(solution)/shard_map/reshape | solution.py:560
  55.6 0.6 %copy.8 = f32[10,16]{1,0:T(8,128)} copy(f32[10,16]{1,0:T(8,128)S(1)} %get-tuple-element.9) | data formatting | bytes 1280

commit v4 on v3

--- a/solution.py
+++ b/solution.py
@@ -15,6 +15,7 @@
 UNITS = 16
 PARTS = 6
 LANES = 128
+LATE = 6
 
 
 def iota(shape, dim):
@@ -41,7 +42,7 @@
 
 def kernel(
     sky_in, leg_ref, own_in, table_in, twid_in, harm_ref, spec_ref,
-    sky_ref, own_ref, table_ref, twid_ref, legv, sendb, recvb, perm, hot, amat, fx, fz, fre, fown, fkeep, fsend, frecv,
+    sky_ref, own_ref, table_ref, twid_ref, legv, sendb, recvb, perm, amat, fx, fz, fre, fown, fkeep, fsend, frecv,
     acc, passb, passr, acc2, s2, r2, t2, q2, acc3, s3, r3, sp, rsp, morder, mweight,
     in_sem, leg_sem, a_send, a_recv, f_send, f_recv, b_send, b_recv, c_send, c_recv,
     h_send, h_recv, d_send, d_recv, e_send, e_recv,
@@ -65,8 +66,9 @@
     def at(axis, v1, v2, v3, cc):
         return device(pick(axis, v1, v3, v2), pick(axis, v2, v1, v3), pick(axis, v3, v2, v1), cc)
 
-    def part_of(u):
-        part = u % PARTS
+    def part_of(u, c=core):
+        late = jnp.where(u == 12, 0, jnp.where(u == 13, 1 + 2 * c, jnp.where(u == 14, 2, 4 + c)))
+        part = jnp.where(u < 12, u % PARTS, late)
         return part, part // 2, part % 2
 
     def pairs(axis, par):
@@ -114,56 +116,60 @@
     for copy in inputs[1:]:
         copy.start()
     loop(PARTS, UNITS, lambda u: leg_copy(u).start())
-    inputs[0].wait()
-
-    def hot_rows(i):
-        rows = pl.ds(pl.multiple_of(i * 128, 128), 128)
-        same = iota((128, 512), 0) + i * 128 == own_ref[...]
-        hot[rows, :] = jnp.where(same, 1.0, 0.0).astype(BF16)
-
-    loop(0, 4, hot_rows)
 
     def perm_rows(axis):
         a1, a2, a3 = coords(axis)
         i = iota((512, 128), 0)
         v3 = (a3 + ((i >> 2) + 1) * (1 - 2 * (a3 % 2)) + 512) & 3
         v2 = (a2 + ((i >> 4) + 1) * (1 - 2 * (a2 % 2)) + 128) & 3
-        v1 = (a1 + ((i >> 7) + 1) * (1 - 2 * (a1 % 2)) + 16) & 3
-        cc = core ^ ((i >> 6) & 1)
+        v1 = (a1 + (((i >> 6) & 3) + 1) * (1 - 2 * (a1 % 2)) + 16) & 3
+        cc = core ^ (i >> 8)
         xx, yy, zz = ((v1, v2, v3), (v3, v1, v2), (v2, v3, v1))[axis]
         slot = (xx << 7) + (yy << 5) + ((zz & 1) << 4) + (cc << 3) + ((zz >> 1) << 2) + (i & 3)
         slot = slot - iota((512, 128), 1)
         chosen = jnp.concatenate(
             [jnp.where(slot == k * 128, 1.0, 0.0).astype(BF16) for k in range(4)], axis=1
         )
-        rows = lax.dot_general(
-            chosen, hot[...], (((1,), (1,)), ((), ())), preferred_element_type=F32
+        if axis == 0:
+            inputs[0].wait()
+        order = own_ref[...]
+        row = iota((8, 512), 0)
+        digits = jnp.where(row == 0, order & 255, jnp.where(row == 1, order >> 8, 0))
+        codes = lax.dot_general(
+            chosen, digits.astype(F32).astype(BF16), (((1,), (1,)), ((), ())),
+            preferred_element_type=F32,
         )
-        perm[axis] = rows.astype(BF16)
+        orders_of = codes[:, 0:1] + 256.0 * codes[:, 1:2]
+        for k in range(4):
+            m = (iota((512, 128), 1) + k * 128).astype(F32)
+            perm[axis, :, k * 128 : k * 128 + 128] = jnp.where(m == orders_of, 1.0, 0.0).astype(BF16)
 
     def a_copies(u):
         part, axis, par = part_of(u)
         a1, a2, a3, first, _ = pairs(axis, par)
+        _, axis_o, par_o = part_of(u, 1 - core)
+        _, b2, b3, first_o, _ = pairs(axis_o, par_o)
         sem = a_recv.at[u]
         return (
             remote(sendb.at[u, 0, pl.ds(0, 2)], recvb.at[u, 1], a_send, sem,
                    at(axis, first, a2, a3, core)),
             remote(sendb.at[u, 1, pl.ds(0, 2)], recvb.at[u, 2], a_send, sem,
-                   at(axis, first, a2, a3, 1 - core)),
+                   at(axis_o, first_o, b2, b3, 1 - core)),
             remote(sendb.at[u, 1, pl.ds(2, 2)], recvb.at[u, 0], a_send, sem,
-                   at(axis, a1, a2, a3, 1 - core)),
+                   device(x, y, z, 1 - core)),
         )
 
     def a_rows(u):
-        part, axis, par = part_of(u)
         leg_copy(u).wait()
-        roles = (3 * par, 1, 3 - 3 * par, 2)
+        kinds = [part_of(u, core), part_of(u, 1 - core)]
         for pair in range(2):
             wide = jnp.concatenate([legv[u, 2 * pair], legv[u, 2 * pair + 1]], axis=1)
-            rows = jnp.dot(perm[axis], wide, preferred_element_type=F32).astype(BF16)
-            for rel in range(4):
-                for rc in range(2):
-                    piece = rows[rel * 128 + rc * 64 : rel * 128 + rc * 64 + 64]
+            for rc, (_, axis, par) in enumerate(kinds):
+                roles = (3 * par, 1, 3 - 3 * par, 2)
+                chosen = perm[axis, rc * 256 : rc * 256 + 256, :]
+                rows = jnp.dot(chosen, wide, preferred_element_type=F32).astype(BF16)
+                for rel in range(4):
+                    piece = rows[rel * 64 : rel * 64 + 64]
                     sendb[u, rc, roles[rel], 2 * pair] = piece[:, :128]
                     sendb[u, rc, roles[rel], 2 * pair + 1] = piece[:, 128:]
 
@@ -241,10 +247,11 @@
             tile = [cols[:, k * 128 : k * 128 + 128] for k in range(4)]
             turned = [pltpu.roll(t, 64, 1) for t in tile]
 
+            def half(rel, rc, side):
+                return (tile if rel % 2 == side else turned)[2 * rc + rel // 2]
+
             def joined(mine, passed, rc):
-                if rc == 0:
-                    return jnp.where(low, tile[mine], turned[passed]).astype(BF16)
-                return jnp.where(low, turned[mine], tile[passed]).astype(BF16)
+                return jnp.where(low, half(mine, rc, 0), half(passed, rc, 1)).astype(BF16)
 
             for par in range(2):
                 part = 2 * axis + par
@@ -301,8 +308,8 @@
 
     def second_axis(u):
         part, axis, par = part_of(u)
-        late = u >= 12
-        return jnp.where(axis == 0, jnp.where(late, 0, 1), jnp.where(axis == 1, jnp.where(late, 1, 0), par))
+        late = jnp.where(u >= LATE, 1, 0)
+        return jnp.where(axis == 0, 1 - late, jnp.where(axis == 1, late, par))
 
     def to_second(u, v, sign):
         part, axis, par = part_of(u)
@@ -321,7 +328,7 @@
         return at(axis, a1, jnp.where(swap == 0, a2, new), jnp.where(swap == 0, new, a3), core)
 
     def turn(u):
-        return (u + u // PARTS) % 2
+        return (part_of(u)[2] + u // PARTS) % 2
 
     def c_copy(u):
         return remote(s2.at[u], r2.at[u], c_send, c_recv.at[u], to_second(u, 1, 1 - 2 * turn(u)))
@@ -378,8 +385,7 @@
 
     pair_rows = [(0, 0), (1, 0), (2, 0), (1, 6), (0, 2), (1, 2), (2, 2), (0, 4), (1, 4), (0, 6)]
 
-    def phase_e(u):
-        all_in(r3.at[u], d_recv.at[u])
+    def e_sums(u):
         total = acc3[u]
         for d in range(3):
             total = total + r3[u, d].astype(F32)
@@ -407,11 +413,28 @@
             for half in range(2):
                 sp[u, k, half : half + 1, :] = packed[half][7 - k : 8 - k]
 
-        for k in range(8):
-
-            @pl.when(u * 8 + k != me)
-            def _():
+    def e_start(u):
+        @pl.when(u != me // 8)
+        def _():
+            for k in range(8):
                 e_copy(u, k).start()
+
+        @pl.when(u == me // 8)
+        def _():
+            def send(k):
+                @pl.when(k != me % 8)
+                def _():
+                    e_copy(u, k).start()
+
+            loop(0, 8, send)
+
+    def phase_e(lo, hi):
+        for u in range(lo, hi):
+            all_in(r3.at[u], d_recv.at[u])
+        for u in range(lo, hi):
+            e_sums(u)
+        for u in range(lo, hi):
+            e_start(u)
 
     def finish():
         arrived = remote(rsp, rsp, e_send, e_recv, device(x, y, z, 1 - core))
@@ -431,7 +454,7 @@
         arrived.wait_send()
 
     def orders():
-        mine = perm[0, 432:448, :].astype(F32)
+        mine = perm[0, 240:256, :].astype(F32)
         m = jnp.sum(mine * iota((16, 512), 1).astype(F32), axis=1, keepdims=True)
         m = jnp.broadcast_to(m, (16, 128))
         full = jnp.concatenate(
@@ -459,35 +482,36 @@
     with jax.named_scope("fourier"):
         fourier()
         f_start()
-    phase("a1", 6, 12, phase_a)
+    phase("a1", 6, 7, phase_a)
+    phase_a(8)
+    phase_a(7)
+    phase("a2", 9, 16, phase_a)
+    with jax.named_scope("orders"):
+        orders()
     with jax.named_scope("build"):
         for part in range(PARTS):
             build(part)
-    phase("bX0", 0, 6, phase_b)
-    phase("aX2", 12, 16, phase_a)
-    phase("bZ1", 10, 12, phase_b)
-    phase("bX1", 6, 10, phase_b)
-    with jax.named_scope("orders"):
-        orders()
+    phase("b0", 0, 6, phase_b)
+    phase("b1", 6, 12, phase_b)
+    phase("bX2", 12, 16, phase_b)
     phase("cX0", 0, 4, phase_c)
-    phase("bX2", 12, 16, phase_b)
     phase("cZ0", 4, 6, phase_c)
+    phase("cX1", 6, 10, phase_c)
     phase("cZ1", 10, 12, phase_c)
+    phase("cX2", 12, 16, phase_c)
     phase("hX0", 0, 4, phase_h)
-    phase("cX1", 6, 10, phase_c)
-    phase("cX2", 12, 16, phase_c)
-    phase("hX1", 6, 10, phase_h)
     phase("hZ0", 4, 6, phase_h)
     phase("hZ1", 10, 12, phase_h)
+    phase("hX1", 6, 10, phase_h)
+    phase("hX2", 12, 16, phase_h)
     phase("dX0", 0, 4, phase_d)
-    phase("hX2", 12, 16, phase_h)
-    phase("dX1", 6, 10, phase_d)
     phase("dZ0", 4, 6, phase_d)
     phase("dZ1", 10, 12, phase_d)
-    phase("eX0", 0, 4, phase_e)
+    phase("dX1", 6, 10, phase_d)
     phase("dX2", 12, 16, phase_d)
-    phase("e1", 4, 12, phase_e)
-    phase("e2", 12, 16, phase_e)
+    for name, lo, hi in (("eX0", 0, 4), ("eZ0", 4, 6), ("eX1", 6, 10), ("eZ1", 10, 12), ("eX2", 12, 16)):
+        with jax.named_scope(name):
+            phase_e(lo, hi)
     with jax.named_scope("finish"):
         finish()
 
@@ -523,7 +547,6 @@
             V((UNITS, 2, 4, 4, 64, 128), BF16),
             V((UNITS, 3, 2, 4, 64, 128), BF16),
             V((3, 512, 512), BF16),
-            V((512, 512), BF16),
             V((PARTS, 8, 128, 256), BF16),
             V((512, 128), F32),
             V((512, 1024), F32),

time: 56.4 us -> 55.5 us (0.984)
  Pallas kernels: 54.2 us -> 53.3 us
    pallas_call x1, Pallas kernels: 54.2 us -> 53.3 us  [per_device(): pl.pallas_call(kernel, out_shape=(jax.ShapeDtypeStruct((32, 2048), F32),...]
where the time goes in v4:
time: 55.5 us; the launch traced here: 55.4 us
  Pallas kernels  53.3 us (96%)
  local copies, waits for them, and re-layouts  1.45 us (3%)
  between operations  0.64 us (1%)
    pallas_call x1, Pallas kernels, per_device(): pl.pallas_call(kernel, out_shape=(jax.ShapeDtypeStruct((32, 2048), F32),...  53.3 us

profile of v4, /device:TPU:7, one launch (start us, length us, event | category | flops | bytes accessed | tf_op | source)
XLA Modules:
  0.0 55.4 jit_solution(7808821810827370242)
XLA Ops:
  0.6 53.3 %analysis.1 = (f32[32,2048]{1,0:T(8,128)S(1)}, f32[10,16]{1,0:T(8,128)S(1)}) custom-call(f32[4,4,4096]{2,1,0:T(4,128)} %sky_in.1, bf16[4,512,2048]{2,1,0:T(8,128)(2,1)} %leg_ref.1, s32[1,512]{1,0:T(1,128)} %bitcast.1, bf16[512,1024]{1,0:T(8,128)(2,1)} %constant.4.clone.table_in, f32[32,2,512]{2,1,0:T(2,128)} %constant.5.clone.twid_in), custom_call_target="tpu_custom_call" | custom-call | tf_op jit(solution)/shard_map/analysis/pallas_call | solution.py:533
  54.0 0.8 %reshape.11 = f32[4,4,2,2048]{3,2,1,0:T(2,128)} reshape(f32[32,2048]{1,0:T(8,128)S(1)} %get-tuple-element.4) | data formatting | bytes 524288 | tf_op jit(solution)/shard_map/reshape | solution.py:583
  54.8 0.6 %copy.8 = f32[10,16]{1,0:T(8,128)} copy(f32[10,16]{1,0:T(8,128)S(1)} %get-tuple-element.9) | data formatting | bytes 1280

commit v5 on v4

--- a/solution.py
+++ b/solution.py
@@ -207,7 +207,8 @@
                 preferred_element_type=F32,
             ) + jnp.dot(high, table_ref[128:256, :], preferred_element_type=F32)
 
-        loop(0, 4, rows_of)
+        for i in range(4):
+            rows_of(i)
 
         def add(k1, sums):
             re, im = sums
@@ -219,7 +220,7 @@
             return re + (zr * c + zi * s), im + (zi * c - zr * s)
 
         zero = jnp.zeros((16, 512), F32)
-        re, im = lax.fori_loop(0, 32, add, (zero, zero))
+        re, im = lax.fori_loop(0, 32, add, (zero, zero), unroll=8)
         fre[0] = re
         fre[1] = im
         for r in range(4):
@@ -433,8 +434,9 @@
             all_in(r3.at[u], d_recv.at[u])
         for u in range(lo, hi):
             e_sums(u)
-        for u in range(lo, hi):
-            e_start(u)
+            if u % 2:
+                e_start(u - 1)
+                e_start(u)
 
     def finish():
         arrived = remote(rsp, rsp, e_send, e_recv, device(x, y, z, 1 - core))
@@ -479,17 +481,17 @@
         phase_a(3)
         perm_rows(2)
         loop(4, 6, phase_a)
+    phase_a(6)
+    phase_a(8)
     with jax.named_scope("fourier"):
         fourier()
         f_start()
-    phase("a1", 6, 7, phase_a)
-    phase_a(8)
     phase_a(7)
     phase("a2", 9, 16, phase_a)
     with jax.named_scope("orders"):
         orders()
     with jax.named_scope("build"):
-        for part in range(PARTS):
+        for part in (1, 3, 4, 5, 0, 2):
             build(part)
     phase("b0", 0, 6, phase_b)
     phase("b1", 6, 12, phase_b)

time: 55.5 us -> 55.3 us (level)
  no operation moved by 1% of the time
where the time goes in v5:
time: 55.3 us; the launch traced here: 55.2 us
  Pallas kernels  53.1 us (96%)
  local copies, waits for them, and re-layouts  1.45 us (3%)
  between operations  0.64 us (1%)
    pallas_call x1, Pallas kernels, per_device(): pl.pallas_call(kernel, out_shape=(jax.ShapeDtypeStruct((32, 2048), F32),...  53.1 us

profile of v5, /device:TPU:7, one launch (start us, length us, event | category | flops | bytes accessed | tf_op | source)
XLA Modules:
  0.0 55.2 jit_solution(5657121095915570883)
XLA Ops:
  0.6 53.1 %analysis.1 = (f32[32,2048]{1,0:T(8,128)S(1)}, f32[10,16]{1,0:T(8,128)S(1)}) custom-call(f32[4,4,4096]{2,1,0:T(4,128)} %sky_in.1, bf16[4,512,2048]{2,1,0:T(8,128)(2,1)} %leg_ref.1, s32[1,512]{1,0:T(1,128)} %bitcast.1, bf16[512,1024]{1,0:T(8,128)(2,1)} %constant.4.clone.table_in, f32[32,2,512]{2,1,0:T(2,128)} %constant.5.clone.twid_in), custom_call_target="tpu_custom_call" | custom-call | tf_op jit(solution)/shard_map/analysis/pallas_call | solution.py:535
  53.7 0.8 %reshape.11 = f32[4,4,2,2048]{3,2,1,0:T(2,128)} reshape(f32[32,2048]{1,0:T(8,128)S(1)} %get-tuple-element.4) | data formatting | bytes 524288 | tf_op jit(solution)/shard_map/reshape | solution.py:585
  54.6 0.6 %copy.8 = f32[10,16]{1,0:T(8,128)} copy(f32[10,16]{1,0:T(8,128)S(1)} %get-tuple-element.9) | data formatting | bytes 1280

commit v6 on v5

--- a/solution.py
+++ b/solution.py
@@ -292,7 +292,7 @@
     def phase_b(u):
         part, axis, par = part_of(u)
         all_in(recvb.at[u], a_recv.at[u])
-        for g in range(8):
+        for g in (4, 5, 6, 7, 0, 1, 2, 3):
             sub, low = g // 4, 16 * (g % 4)
             slabs = [sendb[u, 0, 2 + sub, r, low : low + 16, :] for r in range(4)]
             for src in range(3):
@@ -305,7 +305,8 @@
                 acc[u, rows, :] = out
             else:
                 passb[u, rows, :] = out.astype(BF16)
-        b_copy(u).start()
+            if g == 7:
+                b_copy(u).start()
 
     def second_axis(u):
         part, axis, par = part_of(u)

time: 55.3 us -> 55 us (level)
  no operation moved by 1% of the time
where the time goes in v6:
time: 55 us; the launch traced here: 54.9 us
  Pallas kernels  52.8 us (96%)
  local copies, waits for them, and re-layouts  1.45 us (3%)
  between operations  0.64 us (1%)
    pallas_call x1, Pallas kernels, per_device(): pl.pallas_call(kernel, out_shape=(jax.ShapeDtypeStruct((32, 2048), F32),...  52.8 us

profile of v6, /device:TPU:7, one launch (start us, length us, event | category | flops | bytes accessed | tf_op | source)
XLA Modules:
  0.0 54.9 jit_solution(14124713073553842888)
XLA Ops:
  0.6 52.8 %analysis.1 = (f32[32,2048]{1,0:T(8,128)S(1)}, f32[10,16]{1,0:T(8,128)S(1)}) custom-call(f32[4,4,4096]{2,1,0:T(4,128)} %sky_in.1, bf16[4,512,2048]{2,1,0:T(8,128)(2,1)} %leg_ref.1, s32[1,512]{1,0:T(1,128)} %bitcast.1, bf16[512,1024]{1,0:T(8,128)(2,1)} %constant.4.clone.table_in, f32[32,2,512]{2,1,0:T(2,128)} %constant.5.clone.twid_in), custom_call_target="tpu_custom_call" | custom-call | tf_op jit(solution)/shard_map/analysis/pallas_call | solution.py:536
  53.4 0.8 %reshape.11 = f32[4,4,2,2048]{3,2,1,0:T(2,128)} reshape(f32[32,2048]{1,0:T(8,128)S(1)} %get-tuple-element.4) | data formatting | bytes 524288 | tf_op jit(solution)/shard_map/reshape | solution.py:586
  54.3 0.6 %copy.8 = f32[10,16]{1,0:T(8,128)} copy(f32[10,16]{1,0:T(8,128)S(1)} %get-tuple-element.9) | data formatting | bytes 1280
